TPU v7x, 32 devices: a whole 2x2x4 slice. The times are simulated.
32 devices in a mesh: groups: 2 (over x), tm: 2 (over core), slab: 8 (over z, y).
Axes of the slice: x: 2, y: 2, z: 4, core: 2. Of those that a mesh axis runs over, the one named last changes fastest.
Arguments:
- window_states: float32 [8, 64, 16, 512], P('tm', ('groups', 'slab')), parts along dimension 1, may hold values from -6 to 6
- spatial_weight: bfloat16 [320, 144], replicated, may hold values from -0.5 to 0.5
- temporal_weight: bfloat16 [3, 320, 320], replicated, may hold values from -0.1875 to 0.1875
- out_weight: bfloat16 [16, 320], replicated, may hold values from -0.3125 to 0.3125
- time_embed: float32 [1000, 320], replicated, may hold values from -6 to 6
- step_size: float32 [1000], replicated, may hold values from 0.1 to 0.4
- time_index: int32 [48], P('groups'), parts along dimension 0, may hold values from 0 to 999
- slides: int32 [4], P('groups'), parts along dimension 0, may hold values from 1 to 7
Outputs:
- final_states: float32 [8, 64, 16, 512], P('tm', ('groups', 'slab')), parts along dimension 1
There are 2 independent parts, one for each index of `groups`. A program takes and returns all parts, laid end to end along the dimension named above; an argument that names none is the same for every part. Nothing has to cross between parts.
All inputs are finite; a program needn't handle non-finite values.
Results may differ from a plain program's by a relative error of at most 0.002.
Values may be sent and summed in bfloat16 or wider, within the bound.
No kernel may reach another device: no remote copies, remote signals or barrier semaphores. Data moves between devices by JAX's collectives and lax.ppermute only.
A program may use at most 128 MiB of HBM per device.

v0:
```python
import jax
import jax.numpy as jnp
from jax import lax
from jax.sharding import PartitionSpec as P

C = 16
HEIGHT = 16
WIDTH = 32
ITERS = 2


def with_halo(cells, sides, width):
    for axis, dim in sides:
        count = lax.axis_size(axis)
        ends = count - 1
        head = lax.slice_in_dim(cells, 0, width, axis=dim)
        tail = lax.slice_in_dim(cells, cells.shape[dim] - width, cells.shape[dim], axis=dim)
        cells = jnp.concatenate(
            [
                lax.ppermute(tail, axis, [(i, (i + 1) % count) for i in range(ends)]),
                cells,
                lax.ppermute(head, axis, [((i + 1) % count, i) for i in range(ends)]),
            ],
            axis=dim,
        )
    return cells


def carried_in(part, axis, combine, identity):
    place = lax.axis_index(axis)
    gathered = lax.all_gather(part, axis)
    state = jnp.zeros_like(part) + jnp.asarray(identity, part.dtype)

    def one(lap, state):
        return combine(state, lax.dynamic_index_in_dim(gathered, lap, 0, False))

    return lax.fori_loop(0, place, one, state)


def shift_table():
    cells = HEIGHT * WIDTH
    target = jnp.arange(cells, dtype=jnp.int32)
    cell_row = target // WIDTH
    cell_col = target % WIDTH
    source_ids = jnp.arange(cells, dtype=jnp.int32)
    tables = []
    for row_shift in range(3):
        for col_shift in range(3):
            src_row = cell_row + row_shift - 1
            src_col = cell_col + col_shift - 1
            valid_cells = (src_row >= 0) & (src_row < HEIGHT) & (src_col >= 0) & (src_col < WIDTH)
            source = src_row * WIDTH + src_col
            picked = (source_ids[:, None] == source[None, :]) & valid_cells[None, :]
            tables.append(picked)
    return jnp.stack(tables, axis=0).astype(jnp.bfloat16)


def spatial(latent, spatial_weight):
    times, frames = (latent.shape[0], latent.shape[1])
    moved = jnp.einsum("tfcp,spq->tfscq", latent, shift_table(), preferred_element_type=jnp.float32)
    columns = moved.astype(jnp.bfloat16).reshape(times, frames, 9 * C, HEIGHT * WIDTH)
    return jnp.einsum("oc,tfcp->tfop", spatial_weight, columns, preferred_element_type=jnp.float32)


def add_states(earlier, later):
    return earlier + later


def local(
    window_states,
    spatial_weight,
    temporal_weight,
    out_weight,
    time_embed,
    step_size,
    time_index,
    slides,
):
    states = window_states
    local_times = states.shape[0]
    local_frames = states.shape[1]
    time_rank = lax.axis_index("tm")
    time_count = lax.axis_size("tm")
    slab_rank = lax.axis_index("slab")
    slab_count = lax.axis_size("slab")
    offset = jnp.zeros((), jnp.int32)
    for sweep in range(ITERS):
        indices = lax.dynamic_slice_in_dim(
            time_index, offset + time_rank * local_times, local_times
        )
        one_hot = (
            indices[:, None] == jnp.arange(time_embed.shape[0], dtype=jnp.int32)[None, :]
        ).astype(jnp.float32)
        embed = jnp.dot(one_hot, time_embed, precision=lax.Precision.HIGHEST)
        deltas = jnp.dot(one_hot, step_size, precision=lax.Precision.HIGHEST)
        latent = states.astype(jnp.bfloat16)
        widened = with_halo(latent, (("slab", 1),), 1)
        pre = spatial(widened, spatial_weight) + embed[:, None, :, None]
        first = jax.nn.silu(pre).astype(jnp.bfloat16)
        global_frame = slab_rank * local_frames - 1 + jnp.arange(local_frames + 2, dtype=jnp.int32)
        inside = (global_frame >= 0) & (global_frame < local_frames * slab_count)
        framed = jnp.where(inside[None, :, None, None], first, jnp.zeros_like(first))
        middle = jnp.einsum(
            "oc,tfcp->tfop",
            temporal_weight[0],
            framed[:, 0:local_frames],
            preferred_element_type=jnp.float32,
        )
        for lagged in range(1, 3):
            middle = middle + jnp.einsum(
                "oc,tfcp->tfop",
                temporal_weight[lagged],
                framed[:, lagged : lagged + local_frames],
                preferred_element_type=jnp.float32,
            )
        second = jax.nn.silu(middle).astype(jnp.bfloat16)
        drifts = jnp.einsum("ch,tfhp->tfcp", out_weight, second, preferred_element_type=jnp.float32)
        weighted = deltas[:, None, None, None] * drifts
        running = jnp.cumsum(weighted, axis=0)
        summed = running[-1]
        first_state = jnp.where(time_rank == 0, states[0], jnp.zeros_like(states[0]))
        handed = summed + first_state
        carried = carried_in(handed, "tm", add_states, jnp.zeros_like(handed))
        anchor = jnp.where(time_rank == 0, states[0], carried)
        updated = anchor[None] + (running - weighted)
        ending = anchor + summed
        whole, tails = (
            lax.all_gather(updated, "tm", axis=0, tiled=True),
            lax.all_gather(ending[None], "tm", axis=0, tiled=True),
        )
        tail = tails[time_count - 1]
        extended = jnp.concatenate([whole, jnp.broadcast_to(tail[None], whole.shape)], axis=0)
        shift_now = slides[sweep]
        states = lax.dynamic_slice_in_dim(
            extended, shift_now + time_rank * local_times, local_times
        )
        offset = offset + shift_now
    return states


def solution(mesh):
    return jax.shard_map(
        local,
        mesh=mesh,
        in_specs=(
            P("tm", ("groups", "slab"), None, None),
            P(),
            P(),
            P(),
            P(),
            P(),
            P("groups"),
            P("groups"),
        ),
        out_specs=P("tm", ("groups", "slab"), None, None),
        check_vma=False,
    )
```

profile of v0, /device:TPU:19, one launch (start us, length us, event | category | flops | bytes accessed | tf_op | source)
XLA Modules:
  0.0 147.2 jit_solution(11588758929160838910)
XLA Ops:
  7.7 3.1 %collective-permute-start = (bf16[4,1,16,512]{3,2,1,0:T(8,128)(2,1)S(1)}, bf16[4,1,16,512]{3,2,1,0:T(8,128)(2,1)S(1)}, u32[]{:S(2)}, u32[]{:S(2)}) collective-permute-start(bf16[4,1,16,512]{3,2,1,0:T(8,128)(2,1)S(1)} %get-tuple-element.77), channel_id=1, source_target_pairs={{0,1},{1,2},{2,3},{3,4},{4,5},{5,6},{6,7},{8,9},{9,10},{10,11},{11... | collective-permute-start | bytes 196616 | tf_op jit(solution)/shard_map/ppermute | solution.py:20
  10.9 3.0 %collective-permute-start.1 = (bf16[4,1,16,512]{3,2,1,0:T(8,128)(2,1)S(1)}, bf16[4,1,16,512]{3,2,1,0:T(8,128)(2,1)S(1)}, u32[]{:S(2)}, u32[]{:S(2)}) collective-permute-start(bf16[4,1,16,512]{3,2,1,0:T(8,128)(2,1)S(1)} %get-tuple-element.78), channel_id=1, source_target_pairs={{1,0},{2,1},{3,2},{4,3},{5,4},{6,5},{7,6},{9,8},{10,9},{11,10},{12... | collective-permute-start | bytes 196616 | tf_op jit(solution)/shard_map/ppermute | solution.py:22
  26.8 3.7 %convert_bitcast_fusion.1 = bf16[4,6,9,16,512]{4,3,1,0,2:T(8,128)(2,1)S(1)} fusion(pred[9,512,512]{2,1,0:T(8,128)(4,1)} %fusion.85, bf16[4,1,16,512]{3,2,1,0:T(8,128)(2,1)S(1)} %collective-permute-done.1, bf16[4,4,16,512]{3,2,1,0:T(8,128)(2,1)S(1)} %convert_element_type.34, bf16[4,1,16,512]{3,2,1,0:T(8,128)(2,1)S(1)} %collective-permute-done), kind=kOutput, calls=%fused_computation.47 | convolution fusion | flops 1814888448 | bytes 6291456 | tf_op jit(solution)/shard_map/tfcp,spq->tfscq/dot_general | solution.py:60
  31.4 5.9 %broadcast_select_fusion.1 = bf16[4,6,320,512]{3,2,1,0:T(8,128)(2,1)S(1)} fusion(pred[6]{0:T(512)(128)(4,1)S(1)} %compare_and_fusion.2, f32[4,320]{1,0:T(4,128)S(1)} %fusion.115, bf16[4,6,144,512]{3,2,1,0:T(8,128)(2,1)S(1)} %bitcast.171, bf16[320,144]{0,1:T(8,128)(2,1)S(1)} %copy-done.5), kind=kOutput, calls=%fused_computation.31 | convolution fusion | flops 1159987200 | bytes 11500550 | tf_op jit(solution)/shard_map/oc,tfcp->tfop/dot_general | solution.py:62
  37.3 6.2 %fusion.26 = f32[4,4,512,320]{2,3,1,0:T(8,128)} fusion(bf16[4,6,320,512]{3,2,1,0:T(8,128)(2,1)S(1)} %broadcast_select_fusion.1, bf16[3,320,320]{2,1,0:T(8,128)(2,1)S(1)} %copy-done.4), kind=kOutput, calls=%fused_computation.38 | convolution fusion | flops 1677721600 | bytes 15974400 | tf_op jit(solution)/shard_map/oc,tfcp->tfop/dot_general | solution.py:110
  43.7 5.5 %fusion.28 = f32[4,4,512,320]{2,3,1,0:T(8,128)} fusion(bf16[4,6,320,512]{3,2,1,0:T(8,128)(2,1)S(1)} %broadcast_select_fusion.1, bf16[3,320,320]{2,1,0:T(8,128)(2,1)S(1)} %copy-done.4), kind=kOutput, calls=%fused_computation.40 | convolution fusion | flops 1677721600 | bytes 15974400 | tf_op jit(solution)/shard_map/oc,tfcp->tfop/dot_general | solution.py:110
  49.2 10.8 %fusion.53 = f32[4,4,16,512]{3,2,1,0:T(8,128)S(1)} fusion(f32[4,4,512,320]{2,3,1,0:T(8,128)} %fusion.26, f32[4,4,512,320]{2,3,1,0:T(8,128)} %fusion.28, bf16[4,6,320,512]{3,2,1,0:T(8,128)(2,1)} %copy-done.3, f32[4]{0:T(128)S(1)} %convolution_bitcast_fusion.1, bf16[3,320,320]{2,1,0:T(8,128)(2,1)S(1)} %copy-done.4, bf16[16,320]{1,0:T(8,128)(2,1)S(1)} %copy-done.7), kind=kOutput, calls=%fused_computation.53 | convolution fusion | flops 1780088832 | bytes 26997248 | tf_op jit(solution)/shard_map/ch,tfhp->tfcp/dot_general | solution.py:117
  59.9 2.0 %fusion.156 = f32[4,4,16,512]{3,2,1,0:T(8,128)S(1)} fusion(f32[4,4,16,512]{3,2,1,0:T(8,128)S(1)} %fusion.53), kind=kOutput, calls=%fused_computation.184 | output fusion | flops 393216 | bytes 1048576 | tf_op jit(solution)/shard_map/jit(cumsum)/reduce_window_sum | solution.py:119
  62.8 2.9 %all_gather.20 = f32[2,4,16,512]{3,2,1,0:T(8,128)S(1)} all-gather(f32[1,4,16,512]{3,2,1,0:T(8,128)S(1)} %select_add_fusion.1), channel_id=1, replica_groups=mesh['groups'=2,'tm'=2,'slab'=8] {'tm'}, dimensions={0}, use_global_device_ids=true | all-gather | bytes 393216 | tf_op jit(solution)/shard_map/all_gather | solution.py:31
  68.4 2.0 %all-gather = f32[8,16,512]{2,1,0:T(8,128)S(1)} all-gather(f32[4,16,512]{2,1,0:T(8,128)S(1)} %get-tuple-element.73), channel_id=2, replica_groups=mesh['groups'=2,'tm'=2,'slab'=8] {'tm'}, dimensions={0}, use_global_device_ids=true | all-gather | bytes 393216 | tf_op jit(solution)/shard_map/all_gather | solution.py:129
  70.4 6.9 %all-gather.5.cloned.1.call-done = f32[8,4,16,512]{3,2,1,0:T(8,128)} async-done(((f32[4,4,16,512]{3,2,1,0:T(8,128)}), f32[8,4,16,512]{3,2,1,0:T(8,128)}) %all-gather.5.cloned.1.call-update) | async-done | bytes 1048592 | tf_op jit(solution)/shard_map/all_gather | solution.py:128
  77.5 1.9 %fusion.150 = (bf16[4,4,16,512]{3,2,1,0:T(8,128)(2,1)S(1)}, f32[4,4,16,512]{3,2,1,0:T(8,128)}) fusion(s32[]{:T(128)S(6)} %select_n.215, f32[8,4,16,512]{3,2,1,0:T(8,128)S(1)} %broadcast_in_dim.23, f32[8,4,16,512]{3,2,1,0:T(8,128)} %all-gather.5.cloned.1.call-done), kind=kLoop, calls=%fused_computation.179 | loop fusion | flops 262144 | bytes 2883588 | tf_op jit(solution)/shard_map/convert_element_type | solution.py:96
  79.4 3.1 %collective-permute-start.2 = (bf16[4,1,16,512]{3,2,1,0:T(8,128)(2,1)S(1)}, bf16[4,1,16,512]{3,2,1,0:T(8,128)(2,1)S(1)}, u32[]{:S(2)}, u32[]{:S(2)}) collective-permute-start(bf16[4,1,16,512]{3,2,1,0:T(8,128)(2,1)S(1)} %get-tuple-element.75), channel_id=1, source_target_pairs={{0,1},{1,2},{2,3},{3,4},{4,5},{5,6},{6,7},{8,9},{9,10},{10,11},{11... | collective-permute-start | bytes 196616 | tf_op jit(solution)/shard_map/ppermute | solution.py:20
  82.5 3.1 %collective-permute-start.3 = (bf16[4,1,16,512]{3,2,1,0:T(8,128)(2,1)S(1)}, bf16[4,1,16,512]{3,2,1,0:T(8,128)(2,1)S(1)}, u32[]{:S(2)}, u32[]{:S(2)}) collective-permute-start(bf16[4,1,16,512]{3,2,1,0:T(8,128)(2,1)S(1)} %get-tuple-element.76), channel_id=1, source_target_pairs={{1,0},{2,1},{3,2},{4,3},{5,4},{6,5},{7,6},{9,8},{10,9},{11,10},{12... | collective-permute-start | bytes 196616 | tf_op jit(solution)/shard_map/ppermute | solution.py:22
  85.8 1.7 %collective-permute-done.3 = bf16[4,1,16,512]{3,2,1,0:T(8,128)(2,1)S(1)} collective-permute-done((bf16[4,1,16,512]{3,2,1,0:T(8,128)(2,1)S(1)}, bf16[4,1,16,512]{3,2,1,0:T(8,128)(2,1)S(1)}, u32[]{:S(2)}, u32[]{:S(2)}) %collective-permute-start.3) | collective-permute-done | bytes 65568 | tf_op jit(solution)/shard_map/ppermute | solution.py:22
  87.5 3.7 %convert_bitcast_fusion = bf16[4,6,9,16,512]{4,3,1,0,2:T(8,128)(2,1)S(1)} fusion(pred[9,512,512]{2,1,0:T(8,128)(4,1)} %fusion.85, bf16[4,1,16,512]{3,2,1,0:T(8,128)(2,1)S(1)} %collective-permute-done.3, bf16[4,4,16,512]{3,2,1,0:T(8,128)(2,1)S(1)} %get-tuple-element.71, bf16[4,1,16,512]{3,2,1,0:T(8,128)(2,1)S(1)} %collective-permute-done.2), kind=kOutput, calls=%fused_computation.46 | convolution fusion | flops 1814888448 | bytes 6291456 | tf_op jit(solution)/shard_map/tfcp,spq->tfscq/dot_general | solution.py:60
  92.2 5.9 %broadcast_select_fusion = bf16[4,6,320,512]{3,2,1,0:T(8,128)(2,1)S(1)} fusion(pred[6]{0:T(512)(128)(4,1)S(1)} %compare_and_fusion.2, f32[4,320]{1,0:T(4,128)S(1)} %fusion.114, bf16[4,6,144,512]{3,2,1,0:T(8,128)(2,1)S(1)} %bitcast.170, bf16[320,144]{0,1:T(8,128)(2,1)S(1)} %copy-done.6), kind=kOutput, calls=%fused_computation.30 | convolution fusion | flops 1159987200 | bytes 11500550 | tf_op jit(solution)/shard_map/oc,tfcp->tfop/dot_general | solution.py:62
  98.1 6.2 %fusion.20 = f32[4,4,512,320]{2,3,1,0:T(8,128)} fusion(bf16[4,6,320,512]{3,2,1,0:T(8,128)(2,1)S(1)} %broadcast_select_fusion, bf16[3,320,320]{2,1,0:T(8,128)(2,1)S(1)} %copy-done.4), kind=kOutput, calls=%fused_computation.32 | convolution fusion | flops 1677721600 | bytes 15974400 | tf_op jit(solution)/shard_map/oc,tfcp->tfop/dot_general | solution.py:110
  104.4 5.5 %fusion.22 = f32[4,4,512,320]{2,3,1,0:T(8,128)} fusion(bf16[4,6,320,512]{3,2,1,0:T(8,128)(2,1)S(1)} %broadcast_select_fusion, bf16[3,320,320]{2,1,0:T(8,128)(2,1)S(1)} %copy-done.4), kind=kOutput, calls=%fused_computation.34 | convolution fusion | flops 1677721600 | bytes 15974400 | tf_op jit(solution)/shard_map/oc,tfcp->tfop/dot_general | solution.py:110
  109.9 10.9 %fusion.63 = f32[4,4,16,512]{3,2,1,0:T(8,128)S(1)} fusion(f32[4,4,512,320]{2,3,1,0:T(8,128)} %fusion.20, f32[4,4,512,320]{2,3,1,0:T(8,128)} %fusion.22, bf16[4,6,320,512]{3,2,1,0:T(8,128)(2,1)} %copy-done.2, f32[4]{0:T(128)S(1)} %convolution_bitcast_fusion, bf16[3,320,320]{2,1,0:T(8,128)(2,1)S(1)} %copy-done.4, bf16[16,320]{1,0:T(8,128)(2,1)S(1)} %copy-done.7), kind=kOutput, calls=%fused_computation.55 | convolution fusion | flops 1780088832 | bytes 26997248 | tf_op jit(solution)/shard_map/ch,tfhp->tfcp/dot_general | solution.py:117
  120.8 2.0 %fusion.157 = f32[4,4,16,512]{3,2,1,0:T(8,128)S(1)} fusion(f32[4,4,16,512]{3,2,1,0:T(8,128)S(1)} %fusion.63), kind=kOutput, calls=%fused_computation.185 | output fusion | flops 393216 | bytes 1048576 | tf_op jit(solution)/shard_map/jit(cumsum)/reduce_window_sum | solution.py:119
  123.7 3.3 %all_gather.23 = f32[2,4,16,512]{3,2,1,0:T(8,128)S(1)} all-gather(f32[1,4,16,512]{3,2,1,0:T(8,128)S(1)} %select_add_fusion), channel_id=1, replica_groups=mesh['groups'=2,'tm'=2,'slab'=8] {'tm'}, dimensions={0}, use_global_device_ids=true | all-gather | bytes 393216 | tf_op jit(solution)/shard_map/all_gather | solution.py:31
  129.6 2.0 %all-gather.1 = f32[8,16,512]{2,1,0:T(8,128)S(1)} all-gather(f32[4,16,512]{2,1,0:T(8,128)S(1)} %get-tuple-element.69), channel_id=3, replica_groups=mesh['groups'=2,'tm'=2,'slab'=8] {'tm'}, dimensions={0}, use_global_device_ids=true | all-gather | bytes 393216 | tf_op jit(solution)/shard_map/all_gather | solution.py:129
  131.6 7.7 %all-gather.7.cloned.1.call-done = f32[8,4,16,512]{3,2,1,0:T(8,128)} async-done(((f32[4,4,16,512]{3,2,1,0:T(8,128)}), f32[8,4,16,512]{3,2,1,0:T(8,128)}) %all-gather.7.cloned.1.call-update) | async-done | bytes 1048592 | tf_op jit(solution)/shard_map/all_gather | solution.py:128
  (81 shorter events, 23.3 us)
Async XLA Ops:
  6.5 10.5 %copy-start = (f32[1000,320]{0,1:T(8,128)S(1)}, f32[1000,320]{0,1:T(8,128)}, u32[]{:S(2)}) copy-start(f32[1000,320]{0,1:T(8,128)} %param.16) | copy-start | bytes 3840004
  6.5 70.8 %all-gather.5.cloned.1.call-start = ((), (), s32[]{:S(2)}) async-start(), calls=%async_computation | async-start | bytes 1572864 | tf_op jit(solution)/shard_map/all_gather | solution.py:128
  7.7 19.0 %collective-permute-start = (bf16[4,1,16,512]{3,2,1,0:T(8,128)(2,1)S(1)}, bf16[4,1,16,512]{3,2,1,0:T(8,128)(2,1)S(1)}, u32[]{:S(2)}, u32[]{:S(2)}) collective-permute-start(bf16[4,1,16,512]{3,2,1,0:T(8,128)(2,1)S(1)} %get-tuple-element.77), channel_id=1, source_target_pairs={{0,1},{1,2},{2,3},{3,4},{4,5},{5,6},{6,7},{8,9},{9,10},{10,11},{11... | collective-permute-start | bytes 196616 | tf_op jit(solution)/shard_map/ppermute | solution.py:20
  10.9 15.9 %collective-permute-start.1 = (bf16[4,1,16,512]{3,2,1,0:T(8,128)(2,1)S(1)}, bf16[4,1,16,512]{3,2,1,0:T(8,128)(2,1)S(1)}, u32[]{:S(2)}, u32[]{:S(2)}) collective-permute-start(bf16[4,1,16,512]{3,2,1,0:T(8,128)(2,1)S(1)} %get-tuple-element.78), channel_id=1, source_target_pairs={{1,0},{2,1},{3,2},{4,3},{5,4},{6,5},{7,6},{9,8},{10,9},{11,10},{12... | collective-permute-start | bytes 196616 | tf_op jit(solution)/shard_map/ppermute | solution.py:22
  30.5 0.9 copy-start.5
  31.4 5.9 %copy-start.4 = (bf16[3,320,320]{2,1,0:T(8,128)(2,1)S(1)}, bf16[3,320,320]{2,1,0:T(8,128)(2,1)}, u32[]{:S(2)}) copy-start(bf16[3,320,320]{2,1,0:T(8,128)(2,1)} %param.14) | copy-start | bytes 1843204
  37.3 6.4 %copy-start.3 = (bf16[4,6,320,512]{3,2,1,0:T(8,128)(2,1)}, bf16[4,6,320,512]{3,2,1,0:T(8,128)(2,1)S(1)}, u32[]{:S(2)}) copy-start(bf16[4,6,320,512]{3,2,1,0:T(8,128)(2,1)S(1)} %broadcast_select_fusion.1) | copy-start | bytes 23592964
  43.7 5.5 %copy-start.7 = (bf16[16,320]{1,0:T(8,128)(2,1)S(1)}, bf16[16,320]{1,0:T(8,128)(2,1)}, u32[]{:S(2)}) copy-start(bf16[16,320]{1,0:T(8,128)(2,1)} %param.15) | copy-start | bytes 30724
  59.9 25.7 %copy-start.8 = (f32[1000]{0:T(1024)S(1)}, f32[1000]{0:T(1024)}, u32[]{:S(2)}) copy-start(f32[1000]{0:T(1024)} %param.17) | copy-start | bytes 12004
  67.7 71.7 %all-gather.7.cloned.1.call-start = ((), (), s32[]{:S(2)}) async-start(), calls=%async_computation.1 | async-start | bytes 1572864 | tf_op jit(solution)/shard_map/all_gather | solution.py:128
  79.4 6.4 %collective-permute-start.2 = (bf16[4,1,16,512]{3,2,1,0:T(8,128)(2,1)S(1)}, bf16[4,1,16,512]{3,2,1,0:T(8,128)(2,1)S(1)}, u32[]{:S(2)}, u32[]{:S(2)}) collective-permute-start(bf16[4,1,16,512]{3,2,1,0:T(8,128)(2,1)S(1)} %get-tuple-element.75), channel_id=1, source_target_pairs={{0,1},{1,2},{2,3},{3,4},{4,5},{5,6},{6,7},{8,9},{9,10},{10,11},{11... | collective-permute-start | bytes 196616 | tf_op jit(solution)/shard_map/ppermute | solution.py:20
  82.5 5.0 %collective-permute-start.3 = (bf16[4,1,16,512]{3,2,1,0:T(8,128)(2,1)S(1)}, bf16[4,1,16,512]{3,2,1,0:T(8,128)(2,1)S(1)}, u32[]{:S(2)}, u32[]{:S(2)}) collective-permute-start(bf16[4,1,16,512]{3,2,1,0:T(8,128)(2,1)S(1)} %get-tuple-element.76), channel_id=1, source_target_pairs={{1,0},{2,1},{3,2},{4,3},{5,4},{6,5},{7,6},{9,8},{10,9},{11,10},{12... | collective-permute-start | bytes 196616 | tf_op jit(solution)/shard_map/ppermute | solution.py:22
  91.3 0.9 copy-start.6
  98.0 6.4 %copy-start.2 = (bf16[4,6,320,512]{3,2,1,0:T(8,128)(2,1)}, bf16[4,6,320,512]{3,2,1,0:T(8,128)(2,1)S(1)}, u32[]{:S(2)}) copy-start(bf16[4,6,320,512]{3,2,1,0:T(8,128)(2,1)S(1)} %broadcast_select_fusion) | copy-start | bytes 23592964
  109.9 30.5 %copy-start.1 = (f32[1000,320]{0,1:T(8,128)S(1)}, f32[1000,320]{0,1:T(8,128)}, u32[]{:S(2)}) copy-start(f32[1000,320]{0,1:T(8,128)} %param.16) | copy-start | bytes 3840004
Sparse Core Ops, SparseCore 0:
  67.8 9.5 all-gather.4
  129.1 10.2 all-gather.6
where the time goes:
time: 150 us; the launch traced here: 147 us
  matrix products  66.5 us (44%)
  other arithmetic  21.8 us (15%)
  waiting for transfers between devices  16.4 us (11%)
  between operations  15.1 us (10%)
  starting transfers between devices  12.4 us (8%)
  blocking collectives  10.2 us (7%)
  local copies, waits for them, and re-layouts  4.69 us (3%)
    dot_general x4, matrix products, local(): jnp.einsum('oc,tfcp->tfop', temporal_weight[lagged], framed[:, lagged:lag...  23.3 us
    dot_general x2, matrix products, local(): jnp.einsum('ch,tfhp->tfcp', out_weight, second, preferred_element_type=jn...  21.6 us
    all_gather x2, waiting for transfers between devices, local(): lax.all_gather(updated, 'tm', axis=0, tiled=True)  14.7 us
    dot_general x2, matrix products, spatial(): jnp.einsum('oc,tfcp->tfop', spatial_weight, columns, preferred_element_ty...  11.8 us
    dot_general x2, matrix products, spatial(): jnp.einsum('tfcp,spq->tfscq', latent, shift_table(), preferred_element_ty...  7.45 us
    unnamed x8, other arithmetic  7.25 us
    ppermute x2, starting transfers between devices, with_halo(): lax.ppermute(tail, axis, [(i, (i + 1) % count) for i in range(ends)])  6.25 us
    all_gather x2, blocking collectives, carried_in(): gathered = lax.all_gather(part, axis)  6.18 us
  transfers between devices with their start and end apart: 6, of which 3 were waited for; matrix products, arithmetic and copies ran while one was open for 9% of the time, Pallas kernels for 0%

commit v1 on v0

v1 whole, which is shorter than its diff:
```python
import functools

import jax
import jax.numpy as jnp
from jax import lax
from jax.experimental import pallas as pl
from jax.experimental.pallas import tpu as pltpu
from jax.sharding import PartitionSpec as P

HEIGHT = 16
WIDTH = 32
ITERS = 2
HALO = 2
BF = jnp.bfloat16
F32 = jnp.float32
VMEM = pl.BlockSpec(memory_space=pltpu.VMEM)
SMEM = pl.BlockSpec(memory_space=pltpu.SMEM)
ANY = pl.BlockSpec(memory_space=pl.ANY)


def shape(dims, dtype):
    return jax.ShapeDtypeStruct(dims, dtype)


def prepare(index_ref, slides_ref, states_ref, table_ref, low_ref, high_ref, embed_ref, rows, sems):
    times, frames = states_ref.shape[0], states_ref.shape[1]
    first_time = lax.axis_index("tm") * times
    copies = []
    for sweep in range(ITERS):
        offset = first_time if sweep == 0 else first_time + slides_ref[0]
        for i in range(times):
            slot = sweep * times + i
            row = index_ref[offset + i]
            copy = pltpu.make_async_copy(
                table_ref.at[pl.ds(row, 1)], rows.at[pl.ds(slot, 1)], sems.at[slot]
            )
            copy.start()
            copies.append(copy)
    low_ref[...] = states_ref[:, :HALO].astype(BF)
    high_ref[...] = states_ref[:, frames - HALO :].astype(BF)
    for copy in copies:
        copy.wait()
    embed_ref[...] = rows[...].T


def silu_half(half):
    return half + half * jnp.tanh(half)


def columns_of(latent, lane):
    cells = HEIGHT * WIDTH
    col = lane % WIDTH
    zero = jnp.zeros_like(latent)
    left = jnp.where(col > 0, pltpu.roll(latent, 1, 1), zero)
    right = jnp.where(col < WIDTH - 1, pltpu.roll(latent, cells - 1, 1), zero)
    middle = (left, latent, right)
    above = [jnp.where(lane >= WIDTH, pltpu.roll(x, WIDTH, 1), zero) for x in middle]
    below = [jnp.where(lane < cells - WIDTH, pltpu.roll(x, cells - WIDTH, 1), zero) for x in middle]
    return [*above, *middle, *below]


def one_iteration(
    sweep, low, high, latent_of, valid_of, base_of,
    index_ref, slides_ref, step_ref, spatial_ref, temporal_ref, out_weight_ref, embed_ref,
    own_ref, send_ref, spatial_scr, temporal_scr, first_scr, sums_scr,
):
    times = own_ref.shape[0]
    hidden, taps = spatial_ref.shape
    depth = spatial_scr.shape[1]
    extra = depth - taps
    cells = own_ref.shape[3]
    rank = lax.axis_index("tm")
    lane = lax.broadcasted_iota(jnp.int32, (1, cells), 1)
    for lag in range(3):
        temporal_scr[:, lag * hidden : (lag + 1) * hidden] = (temporal_ref[lag].astype(F32) * 0.5).astype(BF)
    spatial_scr[:, :taps] = (spatial_ref[...].astype(F32) * 0.5).astype(BF)
    for frame in range(low, high):
        sums_scr[0, frame - low] = base_of(frame)
    offset = rank * times + (0 if sweep == 0 else slides_ref[0])
    embed_lane = lax.broadcasted_iota(jnp.int32, (1, embed_ref.shape[1]), 1)
    extra_lane = lax.broadcasted_iota(jnp.int32, (1, extra), 1)

    def conv(t, frame):
        pieces = columns_of(latent_of(t, frame), lane)
        pieces.append(jnp.full((extra, cells), valid_of(frame), F32).astype(BF))
        columns = jnp.concatenate(pieces, axis=0)
        half = jnp.dot(spatial_scr[...], columns, preferred_element_type=F32)
        start = (frame - low + 1) * hidden
        first_scr[start : start + hidden, :] = silu_half(half).astype(BF)

    def temporal(frame):
        start = (frame - low) * hidden
        half = jnp.dot(temporal_scr[...], first_scr[start : start + 3 * hidden, :], preferred_element_type=F32)
        return silu_half(half).astype(BF)

    def project(t, frame, second):
        drift = jnp.dot(out_weight_ref[...], second, preferred_element_type=F32)
        delta = step_ref[index_ref[offset + t]]
        sums_scr[t + 1, frame - low] = sums_scr[t, frame - low] + delta * drift

    def one_time(t, carry):
        picked = jnp.where(embed_lane == sweep * times + t, embed_ref[...], 0.0)
        embed = jnp.sum(picked, axis=1, keepdims=True) * 0.5
        rest = embed
        tail = jnp.zeros((hidden, extra), F32)
        for part in range(3):
            piece = rest.astype(BF).astype(F32)
            tail = jnp.where(extra_lane == part, piece, tail)
            rest = rest - piece
        spatial_scr[:, taps:] = tail.astype(BF)
        conv(t, low - 1)
        conv(t, low)
        waiting = None
        for frame in range(low, high):
            conv(t, frame + 1)
            second = temporal(frame)
            if waiting is not None:
                project(t, *waiting)
            waiting = (frame, second)
        project(t, *waiting)
        return carry

    lax.fori_loop(0, times, one_time, 0)
    slide = slides_ref[sweep]
    for j in range(times):
        own_ref[j] = sums_scr[jnp.minimum(j + slide, times)]
        late = jnp.clip(j + slide - times, 0, times)
        send_ref[j] = sums_scr[jnp.where(rank == 0, times, late)]


def edge_flags():
    slab = lax.axis_index("slab")
    return slab > 0, slab < lax.axis_size("slab") - 1


def iteration_one(index_ref, slides_ref, step_ref, spatial_ref, temporal_ref, out_weight_ref, embed_ref,
                  states_ref, left_ref, right_ref, *rest):
    frames = states_ref.shape[1]
    has_left, has_right = edge_flags()
    rank = lax.axis_index("tm")

    def latent_of(t, frame):
        if frame < 0:
            return left_ref[t, frame + HALO]
        if frame >= frames:
            return right_ref[t, frame - frames]
        return states_ref[t, frame].astype(BF)

    def valid_of(frame):
        if frame < 0:
            return jnp.where(has_left, 1.0, 0.0)
        if frame >= frames:
            return jnp.where(has_right, 1.0, 0.0)
        return 1.0

    def base_of(frame):
        state = states_ref[0, frame] if 0 <= frame < frames else latent_of(0, frame).astype(F32)
        return jnp.where(rank == 0, state, 0.0)

    one_iteration(0, -1, frames + 1, latent_of, valid_of, base_of,
                  index_ref, slides_ref, step_ref, spatial_ref, temporal_ref, out_weight_ref, embed_ref, *rest)


def iteration_two(index_ref, slides_ref, step_ref, spatial_ref, temporal_ref, out_weight_ref, embed_ref,
                  mine_ref, other_ref, *rest):
    frames = mine_ref.shape[1] - 2
    has_left, has_right = edge_flags()
    rank = lax.axis_index("tm")

    def latent_of(t, frame):
        state = mine_ref[t, frame + 1] + other_ref[t, frame + 1]
        return (state if 0 <= frame < frames else state * valid_of(frame)).astype(BF)

    def valid_of(frame):
        if frame < 0:
            return jnp.where(has_left, 1.0, 0.0)
        if frame >= frames:
            return jnp.where(has_right, 1.0, 0.0)
        return 1.0

    def base_of(frame):
        return jnp.where(rank == 0, mine_ref[0, frame + 1] + other_ref[0, frame + 1], 0.0)

    one_iteration(1, 0, frames, latent_of, valid_of, base_of,
                  index_ref, slides_ref, step_ref, spatial_ref, temporal_ref, out_weight_ref, embed_ref, *rest)


def local(window_states, spatial_weight, temporal_weight, out_weight, time_embed, step_size, time_index, slides):
    times, frames, channels, cells = window_states.shape
    hidden, taps = spatial_weight.shape
    slabs, ranks = lax.axis_size("slab"), lax.axis_size("tm")
    assert ranks == 2 and frames >= HALO
    extra = 16
    rows = ITERS * times
    low, high, embed = pl.pallas_call(
        prepare,
        out_shape=(
            shape((times, HALO, channels, cells), BF),
            shape((times, HALO, channels, cells), BF),
            shape((hidden, rows), F32),
        ),
        in_specs=[SMEM, SMEM, VMEM, ANY],
        out_specs=(VMEM, VMEM, VMEM),
        scratch_shapes=[pltpu.VMEM((rows, hidden), F32), pltpu.SemaphoreType.DMA((rows,))],
        name="prepare",
    )(time_index, slides, window_states, time_embed)
    from_left = lax.ppermute(high, "slab", [(i, i + 1) for i in range(slabs - 1)])
    from_right = lax.ppermute(low, "slab", [(i + 1, i) for i in range(slabs - 1)])

    def iterate(body, name, count, arrays):
        result = shape((times, count, channels, cells), F32)
        return pl.pallas_call(
            body,
            out_shape=(result, result),
            in_specs=[SMEM, SMEM, SMEM] + [VMEM] * (4 + len(arrays)),
            out_specs=(VMEM, VMEM),
            scratch_shapes=[
                pltpu.VMEM((hidden, taps + extra), BF),
                pltpu.VMEM((hidden, 3 * hidden), BF),
                pltpu.VMEM(((count + 2) * hidden, cells), BF),
                pltpu.VMEM((times + 1, count, channels, cells), F32),
            ],
            name=name,
        )(time_index, slides, step_size, spatial_weight, temporal_weight, out_weight, embed, *arrays)

    swap = [(0, 1), (1, 0)]
    mine, sent = iterate(iteration_one, "first_iteration", frames + 2, (window_states, from_left, from_right))
    other = lax.ppermute(sent, "tm", swap)
    mine, sent = iterate(iteration_two, "second_iteration", frames, (mine, other))
    return mine + lax.ppermute(sent, "tm", swap)


def solution(mesh):
    return jax.shard_map(
        local,
        mesh=mesh,
        in_specs=(
            P("tm", ("groups", "slab"), None, None),
            P(), P(), P(), P(), P(),
            P("groups"),
            P("groups"),
        ),
        out_specs=P("tm", ("groups", "slab"), None, None),
        check_vma=False,
    )
```

time: 150 us -> 58.4 us (0.39); the launches traced: 147 us -> 57.5 us
  matrix products: 66.5 us -> 0 us
  Pallas kernels: 0 us -> 35.1 us
  other arithmetic: 21.8 us -> 1.92 us
  between operations: 15.1 us -> 0.04 us
  blocking collectives: 10.2 us -> 0 us
  waiting for transfers between devices: 16.4 us -> 7.33 us
  starting transfers between devices: 12.4 us -> 7.81 us
    dot_general x14 -> x0, matrix products: 66.5 us -> none  [the longest x4 23.3 us: local(): jnp.einsum('oc,tfcp->tfop', temporal_weight[lagged], framed[:, lagged:lag...]
    pallas_call x0 -> x3, Pallas kernels: none -> 35.1 us  [the longest x2 32.3 us: iterate(): pl.pallas_call(body, out_shape=(result, result), in_specs=[SMEM, SMEM, SM...]
    all_gather x2 -> x0, waiting for transfers between devices: 14.7 us -> none  [local(): lax.all_gather(updated, 'tm', axis=0, tiled=True)]
    all_gather x4 -> x0, blocking collectives: 10.2 us -> none  [the longest x2 6.18 us: carried_in(): gathered = lax.all_gather(part, axis)]
    unnamed x8 -> x0, other arithmetic: 7.25 us -> none
    ppermute x4, waiting for transfers between devices: 1.74 us -> 7.33 us  [the longest x1 3.08 us: local(): lax.ppermute(low, 'slab', [(i + 1, i) for i in range(slabs - 1)])]
    another operation x3 -> x0, other arithmetic: 4.81 us -> none  [the longest x2 3.94 us: local(): running = jnp.cumsum(weighted, axis=0)]
    ppermute x4, starting transfers between devices: 12.4 us -> 7.81 us  [the longest x1 3.15 us: local(): lax.ppermute(high, 'slab', [(i, i + 1) for i in range(slabs - 1)])]
  transfers between devices with their start and end apart: 6 -> 4, of which waited for: 3 -> 4; matrix products, arithmetic and copies ran while one was open for 9% -> 1% of each run, Pallas kernels for 0% -> 0%
where the time goes in v1:
time: 58.4 us; the launch traced here: 57.5 us
  Pallas kernels  35.1 us (60%)
  starting transfers between devices  7.81 us (13%)
  waiting for transfers between devices  7.33 us (13%)
  local copies, waits for them, and re-layouts  5.3 us (9%)
  other arithmetic  1.92 us (3%)
    pallas_call x2, Pallas kernels, iterate(): pl.pallas_call(body, out_shape=(result, result), in_specs=[SMEM, SMEM, SM...  32.3 us
    unnamed x10, local copies, waits for them, and re-layouts  5.3 us
    ppermute x1, starting transfers between devices, local(): lax.ppermute(high, 'slab', [(i, i + 1) for i in range(slabs - 1)])  3.15 us
    ppermute x1, waiting for transfers between devices, local(): lax.ppermute(low, 'slab', [(i + 1, i) for i in range(slabs - 1)])  3.08 us
    ppermute x1, starting transfers between devices, local(): lax.ppermute(low, 'slab', [(i + 1, i) for i in range(slabs - 1)])  3.03 us
    pallas_call x1, Pallas kernels, local(): pl.pallas_call(prepare, out_shape=(shape((times, HALO, channels, cells),...  2.73 us
    ppermute x1, waiting for transfers between devices, local(): other = lax.ppermute(sent, 'tm', swap)  2.12 us
    add x1, other arithmetic, local(): return mine + lax.ppermute(sent, 'tm', swap)  1.92 us
  transfers between devices with their start and end apart: 4, of which 4 were waited for; matrix products, arithmetic and copies ran while one was open for 1% of the time, Pallas kernels for 0%

profile of v1, /device:TPU:19, one launch (start us, length us, event | category | flops | bytes accessed | tf_op | source)
XLA Modules:
  0.0 57.5 jit_solution(938790299118997129)
XLA Ops:
  0.0 2.9 %copy.9.table_ref = f32[1000,320]{1,0:T(8,128)} copy(f32[1000,320]{0,1:T(8,128)} %param.12) | data formatting | bytes 2560000 | tf_op args[4]
  2.9 0.0 copy-start.3
  2.9 2.7 %prepare.1 = (bf16[4,2,16,512]{3,2,1,0:T(8,128)(2,1)}, bf16[4,2,16,512]{3,2,1,0:T(8,128)(2,1)}, f32[320,8]{1,0:T(8,128)}) custom-call(s32[24]{0:T(128)} %index_ref.5, s32[2]{0:T(128)} %slides_ref.5, f32[4,4,16,512]{3,2,1,0:T(8,128)} %states_ref.3, f32[1000,320]{1,0:T(8,128)} %copy.9.table_ref), custom_call_target="tpu_custom_call" | custom-call | tf_op jit(solution)/shard_map/prepare/pallas_call | solution.py:195
  5.7 3.1 %collective-permute-start = (bf16[4,2,16,512]{3,2,1,0:T(8,128)(2,1)}, bf16[4,2,16,512]{3,2,1,0:T(8,128)(2,1)S(1)}, u32[]{:S(2)}, u32[]{:S(2)}) collective-permute-start(bf16[4,2,16,512]{3,2,1,0:T(8,128)(2,1)} %get-tuple-element.13), channel_id=1, source_target_pairs={{0,1},{1,2},{2,3},{3,4},{4,5},{5,6},{6,7},{8,9},{9,10},{10,11},{11... | collective-permute-start | bytes 393224 | tf_op jit(solution)/shard_map/ppermute | solution.py:207
  8.8 3.0 %collective-permute-start.1 = (bf16[4,2,16,512]{3,2,1,0:T(8,128)(2,1)}, bf16[4,2,16,512]{3,2,1,0:T(8,128)(2,1)S(1)}, u32[]{:S(2)}, u32[]{:S(2)}) collective-permute-start(bf16[4,2,16,512]{3,2,1,0:T(8,128)(2,1)} %get-tuple-element.14), channel_id=1, source_target_pairs={{1,0},{2,1},{3,2},{4,3},{5,4},{6,5},{7,6},{9,8},{10,9},{11,10},{12... | collective-permute-start | bytes 393224 | tf_op jit(solution)/shard_map/ppermute | solution.py:208
  11.9 0.0 copy-done.3
  11.9 0.8 %copy.11.spatial_ref = bf16[320,144]{1,0:T(8,128)(2,1)} copy(bf16[320,144]{0,1:T(8,128)(2,1)S(1)} %copy-done.3) | data formatting | bytes 184320 | tf_op args[1]
  12.7 0.4 collective-permute-done.left_ref
  13.0 0.0 copy-start.1
  13.1 3.1 %collective-permute-done.1.right_ref = bf16[4,2,16,512]{3,2,1,0:T(8,128)(2,1)S(1)} collective-permute-done((bf16[4,2,16,512]{3,2,1,0:T(8,128)(2,1)}, bf16[4,2,16,512]{3,2,1,0:T(8,128)(2,1)S(1)}, u32[]{:S(2)}, u32[]{:S(2)}) %collective-permute-start.1) | collective-permute-done | bytes 131104 | tf_op jit(solution)/shard_map/ppermute | solution.py:208
  16.1 0.0 copy-start.2
  16.1 0.0 copy-done.1
  16.1 0.7 %copy-done.2 = bf16[4,2,16,512]{3,2,1,0:T(8,128)(2,1)} copy-done((bf16[4,2,16,512]{3,2,1,0:T(8,128)(2,1)}, bf16[4,2,16,512]{3,2,1,0:T(8,128)(2,1)S(1)}, u32[]{:S(2)}) %copy-start.2) | copy-done | bytes 131096
  16.8 18.0 %first_iteration.1 = (f32[4,6,16,512]{3,2,1,0:T(8,128)}, f32[4,6,16,512]{3,2,1,0:T(8,128)}) custom-call(s32[24]{0:T(128)} %index_ref.5, s32[2]{0:T(128)} %slides_ref.5, f32[1000]{0:T(1024)} %step_ref.3, bf16[320,144]{1,0:T(8,128)(2,1)} %copy.11.spatial_ref, bf16[3,320,320]{2,1,0:T(8,128)(2,1)} %temporal_ref.3, bf16[16,320]{1,0:T(8,128)(2,1)} %out_weight_ref.3, ...), custom_call_target="tpu_custom_call" | custom-call | tf_op jit(solution)/shard_map/first_iteration/pallas_call | solution.py:212
  34.8 1.3 %collective-permute-start.2 = (f32[4,6,16,512]{3,2,1,0:T(8,128)}, f32[4,6,16,512]{3,2,1,0:T(8,128)S(1)}, u32[]{:S(2)}, u32[]{:S(2)}) collective-permute-start(f32[4,6,16,512]{3,2,1,0:T(8,128)} %get-tuple-element.16), channel_id=1, source_target_pairs={{0,8},{8,0},{1,9},{9,1},{2,10},{10,2},{3,11},{11,3},{4,12},{12,4},... | collective-permute-start | bytes 2359304 | tf_op jit(solution)/shard_map/ppermute | solution.py:228
  36.0 2.1 %collective-permute-done.2.other_ref = f32[4,6,16,512]{3,2,1,0:T(8,128)S(1)} collective-permute-done((f32[4,6,16,512]{3,2,1,0:T(8,128)}, f32[4,6,16,512]{3,2,1,0:T(8,128)S(1)}, u32[]{:S(2)}, u32[]{:S(2)}) %collective-permute-start.2) | collective-permute-done | bytes 786464 | tf_op jit(solution)/shard_map/ppermute | solution.py:228
  38.1 0.0 copy-start
  38.1 0.9 %copy-done = f32[4,6,16,512]{3,2,1,0:T(8,128)} copy-done((f32[4,6,16,512]{3,2,1,0:T(8,128)}, f32[4,6,16,512]{3,2,1,0:T(8,128)S(1)}, u32[]{:S(2)}) %copy-start) | copy-done | bytes 786456
  39.1 14.4 %second_iteration.1 = (f32[4,4,16,512]{3,2,1,0:T(8,128)}, f32[4,4,16,512]{3,2,1,0:T(8,128)}) custom-call(s32[24]{0:T(128)} %index_ref.5, s32[2]{0:T(128)} %slides_ref.5, f32[1000]{0:T(1024)} %step_ref.3, bf16[320,144]{1,0:T(8,128)(2,1)} %copy.11.spatial_ref, bf16[3,320,320]{2,1,0:T(8,128)(2,1)} %temporal_ref.3, bf16[16,320]{1,0:T(8,128)(2,1)} %out_weight_ref.3, ...), custom_call_target="tpu_custom_call" | custom-call | tf_op jit(solution)/shard_map/second_iteration/pallas_call | solution.py:212
  53.4 0.4 collective-permute-start.3
  53.8 1.7 %collective-permute-done.3 = f32[4,4,16,512]{3,2,1,0:T(8,128)S(1)} collective-permute-done((f32[4,4,16,512]{3,2,1,0:T(8,128)}, f32[4,4,16,512]{3,2,1,0:T(8,128)S(1)}, u32[]{:S(2)}, u32[]{:S(2)}) %collective-permute-start.3) | collective-permute-done | bytes 524320 | tf_op jit(solution)/shard_map/ppermute | solution.py:230
  55.5 1.9 %add.3 = f32[4,4,16,512]{3,2,1,0:T(8,128)} add(f32[4,4,16,512]{3,2,1,0:T(8,128)} %get-tuple-element.17, f32[4,4,16,512]{3,2,1,0:T(8,128)S(1)} %collective-permute-done.3) | non-fusion elementwise | flops 131072 | bytes 1572864 | tf_op jit(solution)/shard_map/add | solution.py:230
Async XLA Ops:
  2.9 8.9 %copy-start.3 = (bf16[320,144]{0,1:T(8,128)(2,1)S(1)}, bf16[320,144]{0,1:T(8,128)(2,1)}, u32[]{:S(2)}) copy-start(bf16[320,144]{0,1:T(8,128)(2,1)} %param.9) | copy-start | bytes 276484
  5.7 7.4 %collective-permute-start = (bf16[4,2,16,512]{3,2,1,0:T(8,128)(2,1)}, bf16[4,2,16,512]{3,2,1,0:T(8,128)(2,1)S(1)}, u32[]{:S(2)}, u32[]{:S(2)}) collective-permute-start(bf16[4,2,16,512]{3,2,1,0:T(8,128)(2,1)} %get-tuple-element.13), channel_id=1, source_target_pairs={{0,1},{1,2},{2,3},{3,4},{4,5},{5,6},{6,7},{8,9},{9,10},{10,11},{11... | collective-permute-start | bytes 393224 | tf_op jit(solution)/shard_map/ppermute | solution.py:207
  8.8 7.3 %collective-permute-start.1 = (bf16[4,2,16,512]{3,2,1,0:T(8,128)(2,1)}, bf16[4,2,16,512]{3,2,1,0:T(8,128)(2,1)S(1)}, u32[]{:S(2)}, u32[]{:S(2)}) collective-permute-start(bf16[4,2,16,512]{3,2,1,0:T(8,128)(2,1)} %get-tuple-element.14), channel_id=1, source_target_pairs={{1,0},{2,1},{3,2},{4,3},{5,4},{6,5},{7,6},{9,8},{10,9},{11,10},{12... | collective-permute-start | bytes 393224 | tf_op jit(solution)/shard_map/ppermute | solution.py:208
  13.0 3.1 %copy-start.1 = (bf16[4,2,16,512]{3,2,1,0:T(8,128)(2,1)}, bf16[4,2,16,512]{3,2,1,0:T(8,128)(2,1)S(1)}, u32[]{:S(2)}) copy-start(bf16[4,2,16,512]{3,2,1,0:T(8,128)(2,1)S(1)} %collective-permute-done.left_ref) | copy-start | bytes 393220
  16.1 0.7 %copy-start.2 = (bf16[4,2,16,512]{3,2,1,0:T(8,128)(2,1)}, bf16[4,2,16,512]{3,2,1,0:T(8,128)(2,1)S(1)}, u32[]{:S(2)}) copy-start(bf16[4,2,16,512]{3,2,1,0:T(8,128)(2,1)S(1)} %collective-permute-done.1.right_ref) | copy-start | bytes 393220
  34.8 3.4 %collective-permute-start.2 = (f32[4,6,16,512]{3,2,1,0:T(8,128)}, f32[4,6,16,512]{3,2,1,0:T(8,128)S(1)}, u32[]{:S(2)}, u32[]{:S(2)}) collective-permute-start(f32[4,6,16,512]{3,2,1,0:T(8,128)} %get-tuple-element.16), channel_id=1, source_target_pairs={{0,8},{8,0},{1,9},{9,1},{2,10},{10,2},{3,11},{11,3},{4,12},{12,4},... | collective-permute-start | bytes 2359304 | tf_op jit(solution)/shard_map/ppermute | solution.py:228
  38.1 0.9 %copy-start = (f32[4,6,16,512]{3,2,1,0:T(8,128)}, f32[4,6,16,512]{3,2,1,0:T(8,128)S(1)}, u32[]{:S(2)}) copy-start(f32[4,6,16,512]{3,2,1,0:T(8,128)S(1)} %collective-permute-done.2.other_ref) | copy-start | bytes 2359300
  53.4 2.1 %collective-permute-start.3 = (f32[4,4,16,512]{3,2,1,0:T(8,128)}, f32[4,4,16,512]{3,2,1,0:T(8,128)S(1)}, u32[]{:S(2)}, u32[]{:S(2)}) collective-permute-start(f32[4,4,16,512]{3,2,1,0:T(8,128)} %get-tuple-element.18), channel_id=1, source_target_pairs={{0,8},{8,0},{1,9},{9,1},{2,10},{10,2},{3,11},{11,3},{4,12},{12,4},... | collective-permute-start | bytes 1572872 | tf_op jit(solution)/shard_map/ppermute | solution.py:230

commit v2 on v1

v2 whole, which is shorter than its diff:
```python
import jax
import jax.numpy as jnp
from jax import lax
from jax.experimental import pallas as pl
from jax.experimental.pallas import tpu as pltpu
from jax.sharding import PartitionSpec as P

HEIGHT = 16
WIDTH = 32
ITERS = 2
HALO = 2
LANES = 128
EXTRA = 16
BF = jnp.bfloat16
F32 = jnp.float32
MIB = 1 << 20
VMEM = pl.BlockSpec(memory_space=pltpu.VMEM)
SMEM = pl.BlockSpec(memory_space=pltpu.SMEM)
HBM = pl.BlockSpec(memory_space=pltpu.HBM)


def kept(x, space=pltpu.VMEM):
    return pltpu.with_memory_space_constraint(x, space)


def call(body, name, outs, scalars, arrays, scratch, limit):
    return pl.pallas_call(
        body,
        out_shape=tuple(pltpu.VMEM(dims, dtype) for dims, dtype in outs),
        in_specs=[SMEM] * len(scalars) + [VMEM] * len(arrays),
        out_specs=tuple(VMEM for _ in outs),
        scratch_shapes=scratch,
        compiler_params=pltpu.CompilerParams(vmem_limit_bytes=limit * MIB),
        name=name,
    )(*[kept(x, pltpu.SMEM) for x in scalars], *[kept(x) for x in arrays])


def load(states_ref, index_ref, slides_ref, step_ref, *refs):
    count = (len(refs) - 9) // 2
    weights, outs = refs[:count], refs[count : 2 * count]
    states_out, low_ref, high_ref, picks_ref, steps_ref, index_scr, slides_scr, step_scr, sems = refs[2 * count :]
    pairs = [(index_ref, index_scr), (slides_ref, slides_scr), (step_ref, step_scr), (states_ref, states_out)]
    copies = [pltpu.make_async_copy(x, y, sems.at[n]) for n, (x, y) in enumerate(pairs + list(zip(weights, outs)))]
    for copy in copies:
        copy.start()
    for copy in copies[:3]:
        copy.wait()
    times, frames = states_ref.shape[0], states_ref.shape[1]
    first_time = lax.axis_index("tm") * times
    for sweep in range(ITERS):
        offset = first_time if sweep == 0 else first_time + slides_scr[0]
        for i in range(times):
            index = index_scr[offset + i]
            picks_ref[ITERS + sweep * times + i] = index
            steps_ref[sweep * times + i] = step_scr[index]
        picks_ref[sweep] = slides_scr[sweep]
    copies[3].wait()
    low_ref[...] = states_out[:, :HALO].astype(BF)
    high_ref[...] = states_out[:, frames - HALO :].astype(BF)
    for copy in copies[4:]:
        copy.wait()


def silu_half(half):
    return half + half * jnp.tanh(half)


def pack_weights(picks_ref, spatial_ref, temporal_ref, table_ref, spatial_out, temporal_out, last_scr):
    hidden = spatial_out.shape[1]
    taps = spatial_out.shape[2] - EXTRA
    times = spatial_out.shape[0] // ITERS
    steps = table_ref.shape[1]
    full = steps // LANES
    for lag in range(3):
        temporal_out[:, lag * hidden : (lag + 1) * hidden] = (temporal_ref[lag].astype(F32) * 0.5).astype(BF)
    weight = (spatial_ref[...].astype(F32) * 0.5).T.astype(BF)
    if steps % LANES:
        last_scr[:, : steps % LANES] = table_ref[:, full * LANES :]
    lane = lax.broadcasted_iota(jnp.int32, (1, LANES), 1)
    for sweep in range(ITERS):
        for i in range(times):
            index = picks_ref[ITERS + sweep * times + i]
            tile = index // LANES
            start = pl.multiple_of(jnp.minimum(tile, full - 1) * LANES, LANES)
            block = table_ref[:, pl.ds(start, LANES)]
            if steps % LANES:
                block = jnp.where(tile == full, last_scr[...], block)
            place = index - tile * LANES
            whole = pltpu.roll(block, lax.rem(LANES - place, LANES), 1) * 0.5
            rounded = whole.astype(BF).astype(F32)
            rest = pltpu.roll((whole - rounded).astype(BF).astype(F32), 1, 1)
            both = jnp.where(lane == 0, rounded, jnp.where(lane == 1, rest, 0.0))
            slot = sweep * times + i
            spatial_out[slot, :, :taps] = weight
            spatial_out[slot, :, taps:] = both[:, :EXTRA].astype(BF)


def columns_of(latent, valid):
    cells = HEIGHT * WIDTH
    lane = lax.broadcasted_iota(jnp.int32, (1, cells), 1)
    col = lane % WIDTH
    zero = jnp.zeros_like(latent)
    left = jnp.where(col > 0, pltpu.roll(latent, 1, 1), zero)
    right = jnp.where(col < WIDTH - 1, pltpu.roll(latent, cells - 1, 1), zero)
    middle = (left, latent, right)
    above = [jnp.where(lane >= WIDTH, pltpu.roll(x, WIDTH, 1), zero) for x in middle]
    below = [jnp.where(lane < cells - WIDTH, pltpu.roll(x, cells - WIDTH, 1), zero) for x in middle]
    ones = jnp.full((EXTRA, cells), valid, F32).astype(BF)
    return jnp.concatenate([*above, *middle, *below, ones], axis=0)


def stage(sweep, items, latent_of, valid_of, put_first, get_firsts, add_drift, have,
          steps_ref, spatial_ref, temporal_ref, out_weight_ref):
    times = spatial_ref.shape[0] // ITERS
    done = set()

    def convs(t, frame):
        for f in (frame - 1, frame, frame + 1):
            if (t, f) in done or f in have:
                continue
            done.add((t, f))
            half = jnp.dot(spatial_ref[sweep * times + t], columns_of(latent_of(t, f), valid_of(f)),
                           preferred_element_type=F32)
            put_first(t, f, silu_half(half).astype(BF))

    def project(t, frame, second):
        drift = jnp.dot(out_weight_ref[...], second, preferred_element_type=F32)
        add_drift(t, frame, steps_ref[sweep * times + t] * drift)

    waiting = None
    convs(*items[0])
    for n, (t, frame) in enumerate(items):
        if n + 1 < len(items):
            convs(*items[n + 1])
        half = jnp.dot(temporal_ref[...], get_firsts(t, frame), preferred_element_type=F32)
        second = silu_half(half).astype(BF)
        if waiting is not None:
            project(*waiting)
        waiting = (t, frame, second)
    project(*waiting)


def edge_flag(frame, frames):
    slab = lax.axis_index("slab")
    if frame < 0:
        return jnp.where(slab > 0, 1.0, 0.0)
    if frame >= frames:
        return jnp.where(slab < lax.axis_size("slab") - 1, 1.0, 0.0)
    return 1.0


def inner_first(picks_ref, steps_ref, spatial_ref, temporal_ref, table_ref, out_weight_ref, states_ref,
                spatial_out, temporal_out, first_out, sums_out, last_scr):
    times, frames = states_ref.shape[0], states_ref.shape[1]
    hidden = temporal_out.shape[0]
    rank = lax.axis_index("tm")
    pack_weights(picks_ref, spatial_ref, temporal_ref, table_ref, spatial_out, temporal_out, last_scr)
    for frame in range(1, frames - 1):
        sums_out[0, frame - 1] = jnp.where(rank == 0, states_ref[0, frame], 0.0)

    def put_first(t, f, value):
        first_out[t, f * hidden : (f + 1) * hidden, :] = value

    def get_firsts(t, frame):
        return first_out[t, (frame - 1) * hidden : (frame + 2) * hidden, :]

    def add_drift(t, frame, step):
        sums_out[t + 1, frame - 1] = sums_out[t, frame - 1] + step

    stage(0, [(t, f) for t in range(times) for f in range(1, frames - 1)],
          lambda t, f: states_ref[t, f].astype(BF), lambda f: 1.0, put_first, get_firsts, add_drift, (),
          steps_ref, spatial_out, temporal_out, out_weight_ref)


def deliver(slide, times, frame, sums_of, own_ref, send_ref):
    rank = lax.axis_index("tm")
    for j in range(times):
        own_ref[j, frame] = sums_of(jnp.minimum(j + slide, times))
        late = jnp.clip(j + slide - times, 0, times)
        send_ref[j, frame] = sums_of(jnp.where(rank == 0, times, late))


def outer_first(picks_ref, steps_ref, spatial_ref, temporal_ref, out_weight_ref, states_ref,
                left_ref, right_ref, first_ref, inner_ref, own_ref, send_ref, first_scr, sums_scr):
    times, frames = states_ref.shape[0], states_ref.shape[1]
    hidden = temporal_ref.shape[0]
    rank = lax.axis_index("tm")
    outs = [-1, 0, frames - 1, frames]
    halo = [-2, -1, frames, frames + 1]

    def latent_of(t, f):
        return left_ref[t, f + HALO] if f < 0 else right_ref[t, f - frames]

    for n, f in enumerate(outs):
        state = states_ref[0, f] if 0 <= f < frames else latent_of(0, f).astype(F32)
        sums_scr[0, n] = jnp.where(rank == 0, state, 0.0)

    def put_first(t, f, value):
        n = halo.index(f)
        first_scr[t, n * hidden : (n + 1) * hidden, :] = value

    def get_firsts(t, frame):
        parts = []
        for f in (frame - 1, frame, frame + 1):
            if f in halo:
                n = halo.index(f)
                parts.append(first_scr[t, n * hidden : (n + 1) * hidden, :])
            else:
                parts.append(first_ref[t, f * hidden : (f + 1) * hidden, :])
        return jnp.concatenate(parts, axis=0)

    def add_drift(t, frame, step):
        n = outs.index(frame)
        sums_scr[t + 1, n] = sums_scr[t, n] + step

    stage(0, [(t, f) for t in range(times) for f in outs],
          latent_of, lambda f: edge_flag(f, frames), put_first, get_firsts, add_drift, range(frames),
          steps_ref, spatial_ref, temporal_ref, out_weight_ref)
    for f in range(-1, frames + 1):
        sums = (lambda k, n=outs.index(f): sums_scr[k, n]) if f in outs else (lambda k, f=f: inner_ref[k, f - 1])
        deliver(picks_ref[0], times, f + 1, sums, own_ref, send_ref)


def second(picks_ref, steps_ref, spatial_ref, temporal_ref, out_weight_ref, mine_ref, other_ref,
           own_ref, send_ref, first_scr, sums_scr):
    times, frames = own_ref.shape[0], own_ref.shape[1]
    hidden = temporal_ref.shape[0]
    rank = lax.axis_index("tm")

    def state_of(t, f):
        return mine_ref[t, f + 1] + other_ref[t, f + 1]

    def latent_of(t, f):
        state = state_of(t, f)
        return (state if 0 <= f < frames else state * edge_flag(f, frames)).astype(BF)

    for f in range(frames):
        sums_scr[0, f] = jnp.where(rank == 0, state_of(0, f), 0.0)

    def put_first(t, f, value):
        first_scr[t, (f + 1) * hidden : (f + 2) * hidden, :] = value

    def get_firsts(t, frame):
        return first_scr[t, frame * hidden : (frame + 3) * hidden, :]

    def add_drift(t, frame, step):
        sums_scr[t + 1, frame] = sums_scr[t, frame] + step

    stage(1, [(t, f) for t in range(times) for f in range(frames)],
          latent_of, lambda f: edge_flag(f, frames), put_first, get_firsts, add_drift, (),
          steps_ref, spatial_ref, temporal_ref, out_weight_ref)
    for f in range(frames):
        deliver(picks_ref[1], times, f, lambda k, f=f: sums_scr[k, f], own_ref, send_ref)


def local(window_states, spatial_weight, temporal_weight, out_weight, time_embed, step_size, time_index, slides):
    times, frames, channels, cells = window_states.shape
    hidden, taps = spatial_weight.shape
    slabs, ranks = lax.axis_size("slab"), lax.axis_size("tm")
    assert ranks == 2 and frames >= 3 and cells == HEIGHT * WIDTH
    plane = (channels, cells)
    weights = (spatial_weight.T, temporal_weight, time_embed.T, out_weight)
    edge = pltpu.VMEM((times, HALO) + plane, BF)
    *weights, states, low, high, picks, steps = pl.pallas_call(
        load,
        out_shape=(
            *[pltpu.VMEM(x.shape, x.dtype) for x in weights],
            pltpu.VMEM(window_states.shape, F32), edge, edge,
            pltpu.SMEM((ITERS * (times + 1),), jnp.int32), pltpu.SMEM((ITERS * times,), F32),
        ),
        in_specs=[HBM] * (4 + len(weights)),
        out_specs=(*[VMEM] * (3 + len(weights)), SMEM, SMEM),
        scratch_shapes=[
            pltpu.SMEM(time_index.shape, jnp.int32), pltpu.SMEM(slides.shape, jnp.int32),
            pltpu.SMEM(step_size.shape, F32), pltpu.SemaphoreType.DMA((4 + len(weights),)),
        ],
        compiler_params=pltpu.CompilerParams(vmem_limit_bytes=8 * MIB),
        name="load",
    )(*[kept(x, pltpu.HBM) for x in (window_states, time_index, slides, step_size, *weights)])
    spatial, temporal, table, project = weights
    scalars = (picks, steps)
    from_left = lax.ppermute(high, "slab", [(i, i + 1) for i in range(slabs - 1)])
    from_right = lax.ppermute(low, "slab", [(i + 1, i) for i in range(slabs - 1)])
    spatial, temporal, firsts, inner = call(
        inner_first, "inner_first",
        (
            ((ITERS * times, hidden, taps + EXTRA), BF),
            ((hidden, 3 * hidden), BF),
            ((times, frames * hidden, cells), BF),
            ((times + 1, frames - 2) + plane, F32),
        ),
        scalars, (spatial, temporal, table, project, states),
        [pltpu.VMEM((hidden, LANES), F32)], 16,
    )
    wide = ((times, frames + 2) + plane, F32)
    mine, sent = call(
        outer_first, "outer_first", (wide, wide), scalars,
        (spatial, temporal, project, states, from_left, from_right, firsts, inner),
        [pltpu.VMEM((times, 4 * hidden, cells), BF), pltpu.VMEM((times + 1, 4) + plane, F32)], 16,
    )
    swap = [(0, 1), (1, 0)]
    other = lax.ppermute(sent, "tm", swap)
    block = ((times, frames) + plane, F32)
    mine, sent = call(
        second, "second", (block, block), scalars, (spatial, temporal, project, mine, other),
        [pltpu.VMEM((times, (frames + 2) * hidden, cells), BF), pltpu.VMEM((times + 1, frames) + plane, F32)], 24,
    )
    return mine + lax.ppermute(sent, "tm", swap)


def solution(mesh):
    return jax.shard_map(
        local,
        mesh=mesh,
        in_specs=(
            P("tm", ("groups", "slab"), None, None),
            P(), P(), P(), P(), P(),
            P("groups"),
            P("groups"),
        ),
        out_specs=P("tm", ("groups", "slab"), None, None),
        check_vma=False,
    )
```

time: 58.4 us -> 38.6 us (0.66); the launches traced: 57.5 us -> 38.4 us
  Pallas kernels: 35.1 us -> 26.1 us
  local copies, waits for them, and re-layouts: 5.3 us -> 0 us
  waiting for transfers between devices: 7.33 us -> 3.45 us
  other arithmetic: 1.92 us -> 0.88 us
    pallas_call x3 -> x4, Pallas kernels: 35.1 us -> 26.1 us  [the longest x3 24.3 us: call(): pl.pallas_call(body, out_shape=tuple((pltpu.VMEM(dims, dtype) for dims, d...]
    unnamed x10 -> x0, local copies, waits for them, and re-layouts: 5.3 us -> none
    ppermute x1, waiting for transfers between devices: 3.08 us -> 0.01 us  [local(): lax.ppermute(low, 'slab', [(i + 1, i) for i in range(slabs - 1)])]
    add x1, other arithmetic: 1.92 us -> 0.88 us  [local(): return mine + lax.ppermute(sent, 'tm', swap)]
  transfers between devices with their start and end apart: 4 -> 4, of which waited for: 4 -> 2; matrix products, arithmetic and copies ran while one was open for 1% -> 0% of each run, Pallas kernels for 0% -> 16%
where the time goes in v2:
time: 38.6 us; the launch traced here: 38.4 us
  Pallas kernels  26.1 us (68%)
  starting transfers between devices  7.94 us (21%)
  waiting for transfers between devices  3.45 us (9%)
  other arithmetic  0.88 us (2%)
    pallas_call x3, Pallas kernels, call(): pl.pallas_call(body, out_shape=tuple((pltpu.VMEM(dims, dtype) for dims, d...  24.3 us
    ppermute x1, starting transfers between devices, local(): lax.ppermute(high, 'slab', [(i, i + 1) for i in range(slabs - 1)])  3.15 us
    ppermute x1, starting transfers between devices, local(): lax.ppermute(low, 'slab', [(i + 1, i) for i in range(slabs - 1)])  3.03 us
    ppermute x1, waiting for transfers between devices, local(): other = lax.ppermute(sent, 'tm', swap)  1.91 us
    pallas_call x1, Pallas kernels, local(): pl.pallas_call(load, out_shape=(*[pltpu.VMEM(x.shape, x.dtype) for x in w...  1.81 us
    ppermute x1, waiting for transfers between devices, local(): return mine + lax.ppermute(sent, 'tm', swap)  1.54 us
    ppermute x1, starting transfers between devices, local(): other = lax.ppermute(sent, 'tm', swap)  1.31 us
    add x1, other arithmetic, local(): return mine + lax.ppermute(sent, 'tm', swap)  0.88 us
  transfers between devices with their start and end apart: 4, of which 2 were waited for; matrix products, arithmetic and copies ran while one was open for 0% of the time, Pallas kernels for 16%

profile of v2, /device:TPU:19, one launch (start us, length us, event | category | flops | bytes accessed | tf_op | source)
XLA Modules:
  0.0 38.4 jit_solution(5387012908639457244)
XLA Ops:
  0.0 1.8 %load.1 = (bf16[144,320]{1,0:T(8,128)(2,1)S(1)}, bf16[3,320,320]{2,1,0:T(8,128)(2,1)S(1)}, f32[320,1000]{1,0:T(8,128)S(1)}, bf16[16,320]{1,0:T(8,128)(2,1)S(1)},...) custom-call(f32[4,4,16,512]{3,2,1,0:T(8,128)} %states_ref.1, ...), custom_call_target="tpu_custom_call" | custom-call | tf_op jit(solution)/shard_map/load/pallas_call | solution.py:264
  1.8 3.1 %collective-permute-start = (bf16[4,2,16,512]{3,2,1,0:T(8,128)(2,1)S(1)}, bf16[4,2,16,512]{3,2,1,0:T(8,128)(2,1)S(1)}, u32[]{:S(2)}, u32[]{:S(2)}) collective-permute-start(bf16[4,2,16,512]{3,2,1,0:T(8,128)(2,1)S(1)} %get-tuple-element.31), channel_id=1, source_target_pairs={{0,1},{1,2},{2,3},{3,4},{4,5},{5,6},{6,7},{8,9},{9,10},{10,11},{11... | collective-permute-start | bytes 393224 | tf_op jit(solution)/shard_map/ppermute | solution.py:282
  5.0 3.0 %collective-permute-start.1 = (bf16[4,2,16,512]{3,2,1,0:T(8,128)(2,1)S(1)}, bf16[4,2,16,512]{3,2,1,0:T(8,128)(2,1)S(1)}, u32[]{:S(2)}, u32[]{:S(2)}) collective-permute-start(bf16[4,2,16,512]{3,2,1,0:T(8,128)(2,1)S(1)} %get-tuple-element.32), channel_id=1, source_target_pairs={{1,0},{2,1},{3,2},{4,3},{5,4},{6,5},{7,6},{9,8},{10,9},{11,10},{12... | collective-permute-start | bytes 393224 | tf_op jit(solution)/shard_map/ppermute | solution.py:283
  8.0 6.2 %inner_first.1 = (bf16[8,320,160]{2,1,0:T(8,128)(2,1)S(1)}, bf16[320,960]{1,0:T(8,128)(2,1)S(1)}, bf16[4,1280,512]{2,1,0:T(8,128)(2,1)S(1)}, f32[5,2,16,512]{3,2,1,0:T(8,128)S(1)}) custom-call(s32[10]{0:T(128)S(4)} %get-tuple-element.22.picks_ref, f32[8]{0:T(128)S(4)} %get-tuple-element.23.steps_ref, bf16[144,320]{1,0:T(8,128)(2,1)S(1)} %get-tuple-element.24.spatial_ref, ...), custom_call_target="tpu_custom_call" | custom-call | tf_op jit(solution)/shard_map/inner_first/pallas_call | solution.py:27
  14.2 0.0 collective-permute-done.left_ref
  14.2 0.0 collective-permute-done.1.right_ref
  14.2 8.9 %outer_first.1 = (f32[4,6,16,512]{3,2,1,0:T(8,128)S(1)}, f32[4,6,16,512]{3,2,1,0:T(8,128)S(1)}) custom-call(s32[10]{0:T(128)S(4)} %get-tuple-element.22.picks_ref, f32[8]{0:T(128)S(4)} %get-tuple-element.23.steps_ref, bf16[8,320,160]{2,1,0:T(8,128)(2,1)S(1)} %get-tuple-element.29.spatial_ref, bf16[320,960]{1,0:T(8,128)(2,1)S(1)} %get-tuple-element.30.temporal_ref, ...), custom_call_target="tpu_custom_call" | custom-call | tf_op jit(solution)/shard_map/outer_first/pallas_call | solution.py:27
  23.1 1.3 %collective-permute-start.2 = (f32[4,6,16,512]{3,2,1,0:T(8,128)S(1)}, f32[4,6,16,512]{3,2,1,0:T(8,128)S(1)}, u32[]{:S(2)}, u32[]{:S(2)}) collective-permute-start(f32[4,6,16,512]{3,2,1,0:T(8,128)S(1)} %get-tuple-element.36), channel_id=1, source_target_pairs={{0,8},{8,0},{1,9},{9,1},{2,10},{10,2},{3,11},{11,3},{4,12},{12,4},... | collective-permute-start | bytes 2359304 | tf_op jit(solution)/shard_map/ppermute | solution.py:302
  24.4 1.9 %collective-permute-done.2.other_ref = f32[4,6,16,512]{3,2,1,0:T(8,128)S(1)} collective-permute-done((f32[4,6,16,512]{3,2,1,0:T(8,128)S(1)}, f32[4,6,16,512]{3,2,1,0:T(8,128)S(1)}, u32[]{:S(2)}, u32[]{:S(2)}) %collective-permute-start.2) | collective-permute-done | bytes 786464 | tf_op jit(solution)/shard_map/ppermute | solution.py:302
  26.4 9.2 %second.1 = (f32[4,4,16,512]{3,2,1,0:T(8,128)S(1)}, f32[4,4,16,512]{3,2,1,0:T(8,128)S(1)}) custom-call(s32[10]{0:T(128)S(4)} %get-tuple-element.22.picks_ref, f32[8]{0:T(128)S(4)} %get-tuple-element.23.steps_ref, bf16[8,320,160]{2,1,0:T(8,128)(2,1)S(1)} %get-tuple-element.29.spatial_ref, bf16[320,960]{1,0:T(8,128)(2,1)S(1)} %get-tuple-element.30.temporal_ref, ...), custom_call_target="tpu_custom_call" | custom-call | tf_op jit(solution)/shard_map/second/pallas_call | solution.py:27
  35.5 0.4 %collective-permute-start.3 = (f32[4,4,16,512]{3,2,1,0:T(8,128)S(1)}, f32[4,4,16,512]{3,2,1,0:T(8,128)S(1)}, u32[]{:S(2)}, u32[]{:S(2)}) collective-permute-start(f32[4,4,16,512]{3,2,1,0:T(8,128)S(1)} %get-tuple-element.38), channel_id=1, source_target_pairs={{0,8},{8,0},{1,9},{9,1},{2,10},{10,2},{3,11},{11,3},{4,12},{12,4},... | collective-permute-start | bytes 1572872 | tf_op jit(solution)/shard_map/ppermute | solution.py:308
  36.0 1.5 %collective-permute-done.3 = f32[4,4,16,512]{3,2,1,0:T(8,128)S(1)} collective-permute-done((f32[4,4,16,512]{3,2,1,0:T(8,128)S(1)}, f32[4,4,16,512]{3,2,1,0:T(8,128)S(1)}, u32[]{:S(2)}, u32[]{:S(2)}) %collective-permute-start.3) | collective-permute-done | bytes 524320 | tf_op jit(solution)/shard_map/ppermute | solution.py:308
  37.5 0.9 %add.3 = f32[4,4,16,512]{3,2,1,0:T(8,128)} add(f32[4,4,16,512]{3,2,1,0:T(8,128)S(1)} %get-tuple-element.37, f32[4,4,16,512]{3,2,1,0:T(8,128)S(1)} %collective-permute-done.3) | non-fusion elementwise | flops 131072 | bytes 1572864 | tf_op jit(solution)/shard_map/add | solution.py:308
Async XLA Ops:
  1.8 12.4 %collective-permute-start = (bf16[4,2,16,512]{3,2,1,0:T(8,128)(2,1)S(1)}, bf16[4,2,16,512]{3,2,1,0:T(8,128)(2,1)S(1)}, u32[]{:S(2)}, u32[]{:S(2)}) collective-permute-start(bf16[4,2,16,512]{3,2,1,0:T(8,128)(2,1)S(1)} %get-tuple-element.31), channel_id=1, source_target_pairs={{0,1},{1,2},{2,3},{3,4},{4,5},{5,6},{6,7},{8,9},{9,10},{10,11},{11... | collective-permute-start | bytes 393224 | tf_op jit(solution)/shard_map/ppermute | solution.py:282
  5.0 9.2 %collective-permute-start.1 = (bf16[4,2,16,512]{3,2,1,0:T(8,128)(2,1)S(1)}, bf16[4,2,16,512]{3,2,1,0:T(8,128)(2,1)S(1)}, u32[]{:S(2)}, u32[]{:S(2)}) collective-permute-start(bf16[4,2,16,512]{3,2,1,0:T(8,128)(2,1)S(1)} %get-tuple-element.32), channel_id=1, source_target_pairs={{1,0},{2,1},{3,2},{4,3},{5,4},{6,5},{7,6},{9,8},{10,9},{11,10},{12... | collective-permute-start | bytes 393224 | tf_op jit(solution)/shard_map/ppermute | solution.py:283
  23.1 3.2 %collective-permute-start.2 = (f32[4,6,16,512]{3,2,1,0:T(8,128)S(1)}, f32[4,6,16,512]{3,2,1,0:T(8,128)S(1)}, u32[]{:S(2)}, u32[]{:S(2)}) collective-permute-start(f32[4,6,16,512]{3,2,1,0:T(8,128)S(1)} %get-tuple-element.36), channel_id=1, source_target_pairs={{0,8},{8,0},{1,9},{9,1},{2,10},{10,2},{3,11},{11,3},{4,12},{12,4},... | collective-permute-start | bytes 2359304 | tf_op jit(solution)/shard_map/ppermute | solution.py:302
  35.5 2.0 %collective-permute-start.3 = (f32[4,4,16,512]{3,2,1,0:T(8,128)S(1)}, f32[4,4,16,512]{3,2,1,0:T(8,128)S(1)}, u32[]{:S(2)}, u32[]{:S(2)}) collective-permute-start(f32[4,4,16,512]{3,2,1,0:T(8,128)S(1)} %get-tuple-element.38), channel_id=1, source_target_pairs={{0,8},{8,0},{1,9},{9,1},{2,10},{10,2},{3,11},{11,3},{4,12},{12,4},... | collective-permute-start | bytes 1572872 | tf_op jit(solution)/shard_map/ppermute | solution.py:308

commit v3 on v2

--- a/solution.py
+++ b/solution.py
@@ -55,8 +55,11 @@
             steps_ref[sweep * times + i] = step_scr[index]
         picks_ref[sweep] = slides_scr[sweep]
     copies[3].wait()
-    low_ref[...] = states_out[:, :HALO].astype(BF)
-    high_ref[...] = states_out[:, frames - HALO :].astype(BF)
+    for ref, first in ((low_ref, 0), (high_ref, frames - HALO)):
+        edge = states_out[:, first : first + HALO]
+        rounded = edge.astype(BF)
+        ref[:times] = rounded
+        ref[times] = (edge[0] - rounded[0].astype(F32)).astype(BF)
     for copy in copies[4:]:
         copy.wait()
 
@@ -66,36 +69,38 @@
 
 
 def pack_weights(picks_ref, spatial_ref, temporal_ref, table_ref, spatial_out, temporal_out, last_scr):
-    hidden = spatial_out.shape[1]
-    taps = spatial_out.shape[2] - EXTRA
-    times = spatial_out.shape[0] // ITERS
+    hidden = spatial_out.shape[0]
+    taps = spatial_out.shape[1] - EXTRA
+    slots = EXTRA // 2
     steps = table_ref.shape[1]
     full = steps // LANES
-    for lag in range(3):
-        temporal_out[:, lag * hidden : (lag + 1) * hidden] = (temporal_ref[lag].astype(F32) * 0.5).astype(BF)
-    weight = (spatial_ref[...].astype(F32) * 0.5).T.astype(BF)
     if steps % LANES:
         last_scr[:, : steps % LANES] = table_ref[:, full * LANES :]
     lane = lax.broadcasted_iota(jnp.int32, (1, LANES), 1)
-    for sweep in range(ITERS):
-        for i in range(times):
-            index = picks_ref[ITERS + sweep * times + i]
-            tile = index // LANES
-            start = pl.multiple_of(jnp.minimum(tile, full - 1) * LANES, LANES)
-            block = table_ref[:, pl.ds(start, LANES)]
-            if steps % LANES:
-                block = jnp.where(tile == full, last_scr[...], block)
-            place = index - tile * LANES
-            whole = pltpu.roll(block, lax.rem(LANES - place, LANES), 1) * 0.5
-            rounded = whole.astype(BF).astype(F32)
-            rest = pltpu.roll((whole - rounded).astype(BF).astype(F32), 1, 1)
-            both = jnp.where(lane == 0, rounded, jnp.where(lane == 1, rest, 0.0))
-            slot = sweep * times + i
-            spatial_out[slot, :, :taps] = weight
-            spatial_out[slot, :, taps:] = both[:, :EXTRA].astype(BF)
-
-
-def columns_of(latent, valid):
+    inset = taps % LANES
+    embed = jnp.zeros((hidden, LANES), F32)
+    for slot in range(slots):
+        index = picks_ref[ITERS + slot]
+        tile = index // LANES
+        start = pl.multiple_of(jnp.minimum(tile, full - 1) * LANES, LANES)
+        block = table_ref[:, pl.ds(start, LANES)]
+        if steps % LANES:
+            block = jnp.where(tile == full, last_scr[...], block)
+        place = index - tile * LANES
+        shift = lax.rem(inset + slot + LANES - place, LANES)
+        embed = jnp.where(lane == inset + slot, pltpu.roll(block, shift, 1), embed)
+    embed = embed * 0.5
+    rounded = embed.astype(BF).astype(F32)
+    extra = rounded + pltpu.roll(embed - rounded, slots, 1)
+    weight = (spatial_ref[...].astype(F32) * 0.5).T.astype(BF)
+    spatial_out[:, : taps - inset] = weight[:, : taps - inset]
+    spatial_out[:, taps - inset :] = extra[:, : inset + EXTRA].astype(BF)
+    spatial_out[:, taps - inset : taps] = weight[:, taps - inset :]
+    for lag in range(3):
+        temporal_out[:, lag * hidden : (lag + 1) * hidden] = temporal_ref[lag] * 0.5
+
+
+def columns_of(latent, valid, slot):
     cells = HEIGHT * WIDTH
     lane = lax.broadcasted_iota(jnp.int32, (1, cells), 1)
     col = lane % WIDTH
@@ -105,13 +110,14 @@
     middle = (left, latent, right)
     above = [jnp.where(lane >= WIDTH, pltpu.roll(x, WIDTH, 1), zero) for x in middle]
     below = [jnp.where(lane < cells - WIDTH, pltpu.roll(x, cells - WIDTH, 1), zero) for x in middle]
-    ones = jnp.full((EXTRA, cells), valid, F32).astype(BF)
-    return jnp.concatenate([*above, *middle, *below, ones], axis=0)
+    row = lax.broadcasted_iota(jnp.int32, (EXTRA, cells), 0)
+    picks = jnp.where(lax.rem(row, EXTRA // 2) == slot, valid, 0.0).astype(BF)
+    return jnp.concatenate([*above, *middle, *below, picks], axis=0)
 
 
 def stage(sweep, items, latent_of, valid_of, put_first, get_firsts, add_drift, have,
           steps_ref, spatial_ref, temporal_ref, out_weight_ref):
-    times = spatial_ref.shape[0] // ITERS
+    times = EXTRA // 2 // ITERS
     done = set()
 
     def convs(t, frame):
@@ -119,8 +125,8 @@
             if (t, f) in done or f in have:
                 continue
             done.add((t, f))
-            half = jnp.dot(spatial_ref[sweep * times + t], columns_of(latent_of(t, f), valid_of(f)),
-                           preferred_element_type=F32)
+            columns = columns_of(latent_of(t, f), valid_of(f), sweep * times + t)
+            half = jnp.dot(spatial_ref[...], columns, preferred_element_type=F32)
             put_first(t, f, silu_half(half).astype(BF))
 
     def project(t, frame, second):
@@ -177,7 +183,10 @@
     for j in range(times):
         own_ref[j, frame] = sums_of(jnp.minimum(j + slide, times))
         late = jnp.clip(j + slide - times, 0, times)
-        send_ref[j, frame] = sums_of(jnp.where(rank == 0, times, late))
+        sent = sums_of(jnp.where(rank == 0, times, late))
+        send_ref[j, frame] = sent.astype(send_ref.dtype)
+        if send_ref.shape[0] > times and j == 0:
+            send_ref[times, frame] = (sent - sent.astype(BF).astype(F32)).astype(BF)
 
 
 def outer_first(picks_ref, steps_ref, spatial_ref, temporal_ref, out_weight_ref, states_ref,
@@ -192,7 +201,10 @@
         return left_ref[t, f + HALO] if f < 0 else right_ref[t, f - frames]
 
     for n, f in enumerate(outs):
-        state = states_ref[0, f] if 0 <= f < frames else latent_of(0, f).astype(F32)
+        if 0 <= f < frames:
+            state = states_ref[0, f]
+        else:
+            state = latent_of(0, f).astype(F32) + latent_of(times, f).astype(F32)
         sums_scr[0, n] = jnp.where(rank == 0, state, 0.0)
 
     def put_first(t, f, value):
@@ -228,7 +240,10 @@
     rank = lax.axis_index("tm")
 
     def state_of(t, f):
-        return mine_ref[t, f + 1] + other_ref[t, f + 1]
+        rest = other_ref[times, f + 1].astype(F32)
+        if t > 0:
+            rest = rest * jnp.where(rank == 0, 0.0, 1.0)
+        return mine_ref[t, f + 1] + (other_ref[t, f + 1].astype(F32) + rest)
 
     def latent_of(t, f):
         state = state_of(t, f)
@@ -257,10 +272,10 @@
     times, frames, channels, cells = window_states.shape
     hidden, taps = spatial_weight.shape
     slabs, ranks = lax.axis_size("slab"), lax.axis_size("tm")
-    assert ranks == 2 and frames >= 3 and cells == HEIGHT * WIDTH
+    assert ranks == 2 and EXTRA == 2 * ITERS * times and frames >= 3 and cells == HEIGHT * WIDTH
     plane = (channels, cells)
     weights = (spatial_weight.T, temporal_weight, time_embed.T, out_weight)
-    edge = pltpu.VMEM((times, HALO) + plane, BF)
+    edge = pltpu.VMEM((times + 1, HALO) + plane, BF)
     *weights, states, low, high, picks, steps = pl.pallas_call(
         load,
         out_shape=(
@@ -284,7 +299,7 @@
     spatial, temporal, firsts, inner = call(
         inner_first, "inner_first",
         (
-            ((ITERS * times, hidden, taps + EXTRA), BF),
+            ((hidden, taps + EXTRA), BF),
             ((hidden, 3 * hidden), BF),
             ((times, frames * hidden, cells), BF),
             ((times + 1, frames - 2) + plane, F32),
@@ -294,7 +309,7 @@
     )
     wide = ((times, frames + 2) + plane, F32)
     mine, sent = call(
-        outer_first, "outer_first", (wide, wide), scalars,
+        outer_first, "outer_first", (wide, ((times + 1, frames + 2) + plane, BF)), scalars,
         (spatial, temporal, project, states, from_left, from_right, firsts, inner),
         [pltpu.VMEM((times, 4 * hidden, cells), BF), pltpu.VMEM((times + 1, 4) + plane, F32)], 16,
     )

time: 38.6 us -> 37.5 us (0.972)
  Pallas kernels: 26.1 us -> 25.4 us
  starting transfers between devices: 7.94 us -> 7.5 us
    pallas_call x3, Pallas kernels: 24.3 us -> 23.6 us  [call(): pl.pallas_call(body, out_shape=tuple((pltpu.VMEM(dims, dtype) for dims, d...]
    ppermute x1, starting transfers between devices: 1.31 us -> 0.88 us  [local(): other = lax.ppermute(sent, 'tm', swap)]
    ppermute x1, waiting for transfers between devices: 0.01 us -> 0.43 us  [local(): lax.ppermute(low, 'slab', [(i + 1, i) for i in range(slabs - 1)])]
    ppermute x1, waiting for transfers between devices: 1.91 us -> 1.49 us  [local(): other = lax.ppermute(sent, 'tm', swap)]
  transfers between devices with their start and end apart: 4 -> 4, of which waited for: 2 -> 3; matrix products, arithmetic and copies ran while one was open for 0% -> 0% of each run, Pallas kernels for 16% -> 15%
where the time goes in v3:
time: 37.5 us; the launch traced here: 37.3 us
  Pallas kernels  25.4 us (68%)
  starting transfers between devices  7.5 us (20%)
  waiting for transfers between devices  3.45 us (9%)
  other arithmetic  0.87 us (2%)
    pallas_call x3, Pallas kernels, call(): pl.pallas_call(body, out_shape=tuple((pltpu.VMEM(dims, dtype) for dims, d...  23.6 us
    ppermute x1, starting transfers between devices, local(): lax.ppermute(high, 'slab', [(i, i + 1) for i in range(slabs - 1)])  3.15 us
    ppermute x1, starting transfers between devices, local(): lax.ppermute(low, 'slab', [(i + 1, i) for i in range(slabs - 1)])  3.03 us
    pallas_call x1, Pallas kernels, local(): pl.pallas_call(load, out_shape=(*[pltpu.VMEM(x.shape, x.dtype) for x in w...  1.81 us
    ppermute x1, waiting for transfers between devices, local(): return mine + lax.ppermute(sent, 'tm', swap)  1.54 us
    ppermute x1, waiting for transfers between devices, local(): other = lax.ppermute(sent, 'tm', swap)  1.49 us
    ppermute x1, starting transfers between devices, local(): other = lax.ppermute(sent, 'tm', swap)  0.88 us
    add x1, other arithmetic, local(): return mine + lax.ppermute(sent, 'tm', swap)  0.87 us
  transfers between devices with their start and end apart: 4, of which 3 were waited for; matrix products, arithmetic and copies ran while one was open for 0% of the time, Pallas kernels for 15%

profile of v3, /device:TPU:19, one launch (start us, length us, event | category | flops | bytes accessed | tf_op | source)
XLA Modules:
  0.0 37.3 jit_solution(1086826162308259648)
XLA Ops:
  0.0 1.8 %load.1 = (bf16[144,320]{1,0:T(8,128)(2,1)S(1)}, bf16[3,320,320]{2,1,0:T(8,128)(2,1)S(1)}, f32[320,1000]{1,0:T(8,128)S(1)}, bf16[16,320]{1,0:T(8,128)(2,1)S(1)},...) custom-call(f32[4,4,16,512]{3,2,1,0:T(8,128)} %states_ref.1, ...), custom_call_target="tpu_custom_call" | custom-call | tf_op jit(solution)/shard_map/load/pallas_call | solution.py:279
  1.8 3.1 %collective-permute-start = (bf16[5,2,16,512]{3,2,1,0:T(8,128)(2,1)S(1)}, bf16[5,2,16,512]{3,2,1,0:T(8,128)(2,1)S(1)}, u32[]{:S(2)}, u32[]{:S(2)}) collective-permute-start(bf16[5,2,16,512]{3,2,1,0:T(8,128)(2,1)S(1)} %get-tuple-element.31), channel_id=1, source_target_pairs={{0,1},{1,2},{2,3},{3,4},{4,5},{5,6},{6,7},{8,9},{9,10},{10,11},{11... | collective-permute-start | bytes 491528 | tf_op jit(solution)/shard_map/ppermute | solution.py:297
  5.0 3.0 %collective-permute-start.1 = (bf16[5,2,16,512]{3,2,1,0:T(8,128)(2,1)S(1)}, bf16[5,2,16,512]{3,2,1,0:T(8,128)(2,1)S(1)}, u32[]{:S(2)}, u32[]{:S(2)}) collective-permute-start(bf16[5,2,16,512]{3,2,1,0:T(8,128)(2,1)S(1)} %get-tuple-element.32), channel_id=1, source_target_pairs={{1,0},{2,1},{3,2},{4,3},{5,4},{6,5},{7,6},{9,8},{10,9},{11,10},{12... | collective-permute-start | bytes 491528 | tf_op jit(solution)/shard_map/ppermute | solution.py:298
  8.0 5.7 %inner_first.1 = (bf16[320,160]{1,0:T(8,128)(2,1)S(1)}, bf16[320,960]{1,0:T(8,128)(2,1)S(1)}, bf16[4,1280,512]{2,1,0:T(8,128)(2,1)S(1)}, f32[5,2,16,512]{3,2,1,0:T(8,128)S(1)}) custom-call(s32[10]{0:T(128)S(4)} %get-tuple-element.22.picks_ref, f32[8]{0:T(128)S(4)} %get-tuple-element.23.steps_ref, bf16[144,320]{1,0:T(8,128)(2,1)S(1)} %get-tuple-element.24.spatial_ref, ...), custom_call_target="tpu_custom_call" | custom-call | tf_op jit(solution)/shard_map/inner_first/pallas_call | solution.py:27
  13.8 0.0 collective-permute-done.left_ref
  13.8 0.4 %collective-permute-done.1.right_ref = bf16[5,2,16,512]{3,2,1,0:T(8,128)(2,1)S(1)} collective-permute-done((bf16[5,2,16,512]{3,2,1,0:T(8,128)(2,1)S(1)}, bf16[5,2,16,512]{3,2,1,0:T(8,128)(2,1)S(1)}, u32[]{:S(2)}, u32[]{:S(2)}) %collective-permute-start.1) | collective-permute-done | bytes 163872 | tf_op jit(solution)/shard_map/ppermute | solution.py:298
  14.2 8.6 %outer_first.1 = (f32[4,6,16,512]{3,2,1,0:T(8,128)S(1)}, bf16[5,6,16,512]{3,2,1,0:T(8,128)(2,1)S(1)}) custom-call(s32[10]{0:T(128)S(4)} %get-tuple-element.22.picks_ref, f32[8]{0:T(128)S(4)} %get-tuple-element.23.steps_ref, bf16[320,160]{1,0:T(8,128)(2,1)S(1)} %get-tuple-element.29.spatial_ref, bf16[320,960]{1,0:T(8,128)(2,1)S(1)} %get-tuple-element.30.temporal_ref, ...), custom_call_target="tpu_custom_call" | custom-call | tf_op jit(solution)/shard_map/outer_first/pallas_call | solution.py:27
  22.7 0.9 %collective-permute-start.2 = (bf16[5,6,16,512]{3,2,1,0:T(8,128)(2,1)S(1)}, bf16[5,6,16,512]{3,2,1,0:T(8,128)(2,1)S(1)}, u32[]{:S(2)}, u32[]{:S(2)}) collective-permute-start(bf16[5,6,16,512]{3,2,1,0:T(8,128)(2,1)S(1)} %get-tuple-element.36), channel_id=1, source_target_pairs={{0,8},{8,0},{1,9},{9,1},{2,10},{10,2},{3,11},{11,3},{4,12},{12,4},... | collective-permute-start | bytes 1474568 | tf_op jit(solution)/shard_map/ppermute | solution.py:317
  23.6 1.5 %collective-permute-done.2.other_ref = bf16[5,6,16,512]{3,2,1,0:T(8,128)(2,1)S(1)} collective-permute-done((bf16[5,6,16,512]{3,2,1,0:T(8,128)(2,1)S(1)}, bf16[5,6,16,512]{3,2,1,0:T(8,128)(2,1)S(1)}, u32[]{:S(2)}, u32[]{:S(2)}) %collective-permute-start.2) | collective-permute-done | bytes 491552 | tf_op jit(solution)/shard_map/ppermute | solution.py:317
  25.1 9.3 %second.1 = (f32[4,4,16,512]{3,2,1,0:T(8,128)S(1)}, f32[4,4,16,512]{3,2,1,0:T(8,128)S(1)}) custom-call(s32[10]{0:T(128)S(4)} %get-tuple-element.22.picks_ref, f32[8]{0:T(128)S(4)} %get-tuple-element.23.steps_ref, bf16[320,160]{1,0:T(8,128)(2,1)S(1)} %get-tuple-element.29.spatial_ref, bf16[320,960]{1,0:T(8,128)(2,1)S(1)} %get-tuple-element.30.temporal_ref, ...), custom_call_target="tpu_custom_call" | custom-call | tf_op jit(solution)/shard_map/second/pallas_call | solution.py:27
  34.5 0.4 %collective-permute-start.3 = (f32[4,4,16,512]{3,2,1,0:T(8,128)S(1)}, f32[4,4,16,512]{3,2,1,0:T(8,128)S(1)}, u32[]{:S(2)}, u32[]{:S(2)}) collective-permute-start(f32[4,4,16,512]{3,2,1,0:T(8,128)S(1)} %get-tuple-element.38), channel_id=1, source_target_pairs={{0,8},{8,0},{1,9},{9,1},{2,10},{10,2},{3,11},{11,3},{4,12},{12,4},... | collective-permute-start | bytes 1572872 | tf_op jit(solution)/shard_map/ppermute | solution.py:323
  34.9 1.5 %collective-permute-done.3 = f32[4,4,16,512]{3,2,1,0:T(8,128)S(1)} collective-permute-done((f32[4,4,16,512]{3,2,1,0:T(8,128)S(1)}, f32[4,4,16,512]{3,2,1,0:T(8,128)S(1)}, u32[]{:S(2)}, u32[]{:S(2)}) %collective-permute-start.3) | collective-permute-done | bytes 524320 | tf_op jit(solution)/shard_map/ppermute | solution.py:323
  36.4 0.9 %add.3 = f32[4,4,16,512]{3,2,1,0:T(8,128)} add(f32[4,4,16,512]{3,2,1,0:T(8,128)S(1)} %get-tuple-element.37, f32[4,4,16,512]{3,2,1,0:T(8,128)S(1)} %collective-permute-done.3) | non-fusion elementwise | flops 131072 | bytes 1572864 | tf_op jit(solution)/shard_map/add | solution.py:323
Async XLA Ops:
  1.8 11.9 %collective-permute-start = (bf16[5,2,16,512]{3,2,1,0:T(8,128)(2,1)S(1)}, bf16[5,2,16,512]{3,2,1,0:T(8,128)(2,1)S(1)}, u32[]{:S(2)}, u32[]{:S(2)}) collective-permute-start(bf16[5,2,16,512]{3,2,1,0:T(8,128)(2,1)S(1)} %get-tuple-element.31), channel_id=1, source_target_pairs={{0,1},{1,2},{2,3},{3,4},{4,5},{5,6},{6,7},{8,9},{9,10},{10,11},{11... | collective-permute-start | bytes 491528 | tf_op jit(solution)/shard_map/ppermute | solution.py:297
  5.0 9.2 %collective-permute-start.1 = (bf16[5,2,16,512]{3,2,1,0:T(8,128)(2,1)S(1)}, bf16[5,2,16,512]{3,2,1,0:T(8,128)(2,1)S(1)}, u32[]{:S(2)}, u32[]{:S(2)}) collective-permute-start(bf16[5,2,16,512]{3,2,1,0:T(8,128)(2,1)S(1)} %get-tuple-element.32), channel_id=1, source_target_pairs={{1,0},{2,1},{3,2},{4,3},{5,4},{6,5},{7,6},{9,8},{10,9},{11,10},{12... | collective-permute-start | bytes 491528 | tf_op jit(solution)/shard_map/ppermute | solution.py:298
  22.7 2.4 %collective-permute-start.2 = (bf16[5,6,16,512]{3,2,1,0:T(8,128)(2,1)S(1)}, bf16[5,6,16,512]{3,2,1,0:T(8,128)(2,1)S(1)}, u32[]{:S(2)}, u32[]{:S(2)}) collective-permute-start(bf16[5,6,16,512]{3,2,1,0:T(8,128)(2,1)S(1)} %get-tuple-element.36), channel_id=1, source_target_pairs={{0,8},{8,0},{1,9},{9,1},{2,10},{10,2},{3,11},{11,3},{4,12},{12,4},... | collective-permute-start | bytes 1474568 | tf_op jit(solution)/shard_map/ppermute | solution.py:317
  34.5 2.0 %collective-permute-start.3 = (f32[4,4,16,512]{3,2,1,0:T(8,128)S(1)}, f32[4,4,16,512]{3,2,1,0:T(8,128)S(1)}, u32[]{:S(2)}, u32[]{:S(2)}) collective-permute-start(f32[4,4,16,512]{3,2,1,0:T(8,128)S(1)} %get-tuple-element.38), channel_id=1, source_target_pairs={{0,8},{8,0},{1,9},{9,1},{2,10},{10,2},{3,11},{11,3},{4,12},{12,4},... | collective-permute-start | bytes 1572872 | tf_op jit(solution)/shard_map/ppermute | solution.py:323

commit v4 on v3

--- a/solution.py
+++ b/solution.py
@@ -14,6 +14,8 @@
 BF = jnp.bfloat16
 F32 = jnp.float32
 MIB = 1 << 20
+TILE = 256
+PIECE = 64
 VMEM = pl.BlockSpec(memory_space=pltpu.VMEM)
 SMEM = pl.BlockSpec(memory_space=pltpu.SMEM)
 HBM = pl.BlockSpec(memory_space=pltpu.HBM)
@@ -68,9 +70,9 @@
     return half + half * jnp.tanh(half)
 
 
-def pack_weights(picks_ref, spatial_ref, temporal_ref, table_ref, spatial_out, temporal_out, last_scr):
+def pack_weights(picks_ref, spatial_ref, temporal_ref, table_ref, spatial_out, temporal_out, project_ref, project_out, last_scr):
     hidden = spatial_out.shape[0]
-    taps = spatial_out.shape[1] - EXTRA
+    taps = spatial_ref.shape[0]
     slots = EXTRA // 2
     steps = table_ref.shape[1]
     full = steps // LANES
@@ -94,10 +96,14 @@
     extra = rounded + pltpu.roll(embed - rounded, slots, 1)
     weight = (spatial_ref[...].astype(F32) * 0.5).T.astype(BF)
     spatial_out[:, : taps - inset] = weight[:, : taps - inset]
-    spatial_out[:, taps - inset :] = extra[:, : inset + EXTRA].astype(BF)
+    spatial_out[:, taps - inset :] = extra.astype(BF)
     spatial_out[:, taps - inset : taps] = weight[:, taps - inset :]
     for lag in range(3):
         temporal_out[:, lag * hidden : (lag + 1) * hidden] = temporal_ref[lag] * 0.5
+    for ref, used in ((temporal_out, 3 * hidden), (project_out, hidden)):
+        if used < ref.shape[1]:
+            ref[:, used:] = jnp.zeros((ref.shape[0], ref.shape[1] - used), BF)
+    project_out[:, :hidden] = project_ref[...]
 
 
 def columns_of(latent, valid, slot):
@@ -115,35 +121,125 @@
     return jnp.concatenate([*above, *middle, *below, picks], axis=0)
 
 
-def stage(sweep, items, latent_of, valid_of, put_first, get_firsts, add_drift, have,
-          steps_ref, spatial_ref, temporal_ref, out_weight_ref):
+def filled(parts, width):
+    rows = sum(x.shape[0] for x in parts)
+    if rows < TILE:
+        parts = [*parts, jnp.zeros((TILE - rows, width), BF)]
+    return parts[0] if len(parts) == 1 else jnp.concatenate(parts, axis=0)
+
+
+def stage(sweep, items, latent_of, valid_of, put_first, first_at, add_drift, have,
+          steps_ref, spatial_ref, temporal_ref, project_ref):
     times = EXTRA // 2 // ITERS
-    done = set()
-
-    def convs(t, frame):
+    hidden = spatial_ref.shape[0]
+    pieces = hidden // PIECE
+    units = range(2)
+    halves = [slice(q * TILE, (q + 1) * TILE) for q in units]
+    order, needed = [], []
+    for t, frame in items:
         for f in (frame - 1, frame, frame + 1):
-            if (t, f) in done or f in have:
-                continue
-            done.add((t, f))
+            if (t, f) not in order and f not in have:
+                order.append((t, f))
+        needed.append(len(order))
+    last = len(items) - 1
+
+    def run(*accs):
+        per = 3 * pieces + 1
+        sets = [[[accs[q * per + k * pieces + i] for i in range(pieces)] for q in units] for k in range(3)]
+        small = [accs[q * per + 3 * pieces] for q in units]
+        state = {"pass": 0, "issued": 0}
+
+        def one_pass(tiles, outs, lhs_of):
+            register = state["pass"] % 2
+            state["pass"] += 1
+            for q in units:
+                pltpu.matmul_push_rhs(tiles[q], staging_register=register, mxu_index=q)
+            for i in range(len(outs[0])):
+                lhs = lhs_of(i)
+                for q in units:
+                    pltpu.matmul_acc_lhs(outs[q][i], lhs, load_staged_rhs=register if i == 0 else None)
+
+        def conv(into):
+            t, f = order[state["issued"]]
+            state["issued"] += 1
             columns = columns_of(latent_of(t, f), valid_of(f), sweep * times + t)
-            half = jnp.dot(spatial_ref[...], columns, preferred_element_type=F32)
-            put_first(t, f, silu_half(half).astype(BF))
-
-    def project(t, frame, second):
-        drift = jnp.dot(out_weight_ref[...], second, preferred_element_type=F32)
-        add_drift(t, frame, steps_ref[sweep * times + t] * drift)
-
-    waiting = None
-    convs(*items[0])
-    for n, (t, frame) in enumerate(items):
-        if n + 1 < len(items):
-            convs(*items[n + 1])
-        half = jnp.dot(temporal_ref[...], get_firsts(t, frame), preferred_element_type=F32)
-        second = silu_half(half).astype(BF)
-        if waiting is not None:
-            project(*waiting)
-        waiting = (t, frame, second)
-    project(*waiting)
+            tiles = [filled([columns[:, h]], TILE) for h in halves]
+            one_pass(tiles, sets[into], lambda i: spatial_ref[i * PIECE : (i + 1) * PIECE, :])
+            return t, f, into
+
+        def finish_conv(t, f, into):
+            for i in range(pieces):
+                for q in units:
+                    value = silu_half(pltpu.matmul_pop(sets[into][q][i])).astype(BF)
+                    put_first(t, f, value, i * PIECE, halves[q])
+
+        def temporal(n, k):
+            t, frame = items[n]
+            low, high = k * TILE, min((k + 1) * TILE, 3 * hidden)
+            tiles = []
+            for h in halves:
+                parts = []
+                for d in range(3):
+                    start, stop = max(low, d * hidden), min(high, (d + 1) * hidden)
+                    if start < stop:
+                        parts.append(first_at(t, frame - 1 + d, start - d * hidden, stop - d * hidden, h))
+                tiles.append(filled(parts, TILE))
+            one_pass(tiles, sets[n % 2], lambda i: temporal_ref[i * PIECE : (i + 1) * PIECE, low : low + TILE])
+
+        def finish_temporal(n):
+            return [[silu_half(pltpu.matmul_pop(sets[n % 2][q][i])).astype(BF) for i in range(pieces)] for q in units]
+
+        def project(second, k):
+            count = TILE // PIECE
+            tiles = [filled(second[q][k * count : (k + 1) * count], TILE) for q in units]
+            one_pass(tiles, [[x] for x in small], lambda i: project_ref[:, k * TILE : (k + 1) * TILE])
+
+        def finish_project(n):
+            t, frame = items[n]
+            for q in units:
+                add_drift(t, frame, steps_ref[sweep * times + t] * pltpu.matmul_pop(small[q]), halves[q])
+
+        temporal_passes = pl.cdiv(3 * hidden, TILE)
+        project_passes = pl.cdiv(hidden, TILE)
+        assert temporal_passes == 4 and project_passes == 2
+        pending = None
+        for i in range(needed[0]):
+            issued = conv(2 if (needed[0] - 1 - i) % 2 == 0 else 1)
+            if pending is not None:
+                finish_conv(*pending)
+            pending = issued
+        second = None
+        for n in range(len(items)):
+            ahead = needed[min(n + 2, last)]
+            temporal(n, 0)
+            if pending is not None:
+                finish_conv(*pending)
+                pending = None
+            early = conv(2) if state["issued"] < ahead else None
+            temporal(n, 1)
+            if n > 0:
+                second = finish_temporal(n - 1)
+            if n > 1:
+                finish_project(n - 2)
+            temporal(n, 2)
+            if n > 0:
+                project(second, 0)
+            if early is not None:
+                finish_conv(*early)
+            pending = conv(2) if state["issued"] < ahead else None
+            temporal(n, 3)
+            if n > 0:
+                project(second, 1)
+            assert n == last or state["issued"] >= needed[n + 1]
+        second = finish_temporal(last)
+        if last > 0:
+            finish_project(last - 1)
+        project(second, 0)
+        project(second, 1)
+        finish_project(last)
+
+    shapes = [(PIECE, TILE)] * (3 * pieces) + [(project_ref.shape[0], TILE)]
+    pl.run_scoped(run, *[pltpu.ACC(q)(dims, F32) for q in units for dims in shapes])
 
 
 def edge_flag(frame, frames):
@@ -156,26 +252,26 @@
 
 
 def inner_first(picks_ref, steps_ref, spatial_ref, temporal_ref, table_ref, out_weight_ref, states_ref,
-                spatial_out, temporal_out, first_out, sums_out, last_scr):
+                spatial_out, temporal_out, project_out, first_out, sums_out, last_scr):
     times, frames = states_ref.shape[0], states_ref.shape[1]
     hidden = temporal_out.shape[0]
     rank = lax.axis_index("tm")
-    pack_weights(picks_ref, spatial_ref, temporal_ref, table_ref, spatial_out, temporal_out, last_scr)
+    pack_weights(picks_ref, spatial_ref, temporal_ref, table_ref, spatial_out, temporal_out, out_weight_ref, project_out, last_scr)
     for frame in range(1, frames - 1):
         sums_out[0, frame - 1] = jnp.where(rank == 0, states_ref[0, frame], 0.0)
 
-    def put_first(t, f, value):
-        first_out[t, f * hidden : (f + 1) * hidden, :] = value
-
-    def get_firsts(t, frame):
-        return first_out[t, (frame - 1) * hidden : (frame + 2) * hidden, :]
-
-    def add_drift(t, frame, step):
-        sums_out[t + 1, frame - 1] = sums_out[t, frame - 1] + step
+    def put_first(t, f, value, row, half):
+        first_out[t, f * hidden + row : f * hidden + row + PIECE, half] = value
+
+    def first_at(t, f, start, stop, half):
+        return first_out[t, f * hidden + start : f * hidden + stop, half]
+
+    def add_drift(t, frame, step, half):
+        sums_out[t + 1, frame - 1, :, half] = sums_out[t, frame - 1, :, half] + step
 
     stage(0, [(t, f) for t in range(times) for f in range(1, frames - 1)],
-          lambda t, f: states_ref[t, f].astype(BF), lambda f: 1.0, put_first, get_firsts, add_drift, (),
-          steps_ref, spatial_out, temporal_out, out_weight_ref)
+          lambda t, f: states_ref[t, f].astype(BF), lambda f: 1.0, put_first, first_at, add_drift, (),
+          steps_ref, spatial_out, temporal_out, project_out)
 
 
 def deliver(slide, times, frame, sums_of, own_ref, send_ref):
@@ -207,26 +303,22 @@
             state = latent_of(0, f).astype(F32) + latent_of(times, f).astype(F32)
         sums_scr[0, n] = jnp.where(rank == 0, state, 0.0)
 
-    def put_first(t, f, value):
-        n = halo.index(f)
-        first_scr[t, n * hidden : (n + 1) * hidden, :] = value
-
-    def get_firsts(t, frame):
-        parts = []
-        for f in (frame - 1, frame, frame + 1):
-            if f in halo:
-                n = halo.index(f)
-                parts.append(first_scr[t, n * hidden : (n + 1) * hidden, :])
-            else:
-                parts.append(first_ref[t, f * hidden : (f + 1) * hidden, :])
-        return jnp.concatenate(parts, axis=0)
-
-    def add_drift(t, frame, step):
+    def put_first(t, f, value, row, half):
+        start = halo.index(f) * hidden + row
+        first_scr[t, start : start + PIECE, half] = value
+
+    def first_at(t, f, start, stop, half):
+        if f in halo:
+            n = halo.index(f)
+            return first_scr[t, n * hidden + start : n * hidden + stop, half]
+        return first_ref[t, f * hidden + start : f * hidden + stop, half]
+
+    def add_drift(t, frame, step, half):
         n = outs.index(frame)
-        sums_scr[t + 1, n] = sums_scr[t, n] + step
+        sums_scr[t + 1, n, :, half] = sums_scr[t, n, :, half] + step
 
     stage(0, [(t, f) for t in range(times) for f in outs],
-          latent_of, lambda f: edge_flag(f, frames), put_first, get_firsts, add_drift, range(frames),
+          latent_of, lambda f: edge_flag(f, frames), put_first, first_at, add_drift, range(frames),
           steps_ref, spatial_ref, temporal_ref, out_weight_ref)
     for f in range(-1, frames + 1):
         sums = (lambda k, n=outs.index(f): sums_scr[k, n]) if f in outs else (lambda k, f=f: inner_ref[k, f - 1])
@@ -252,17 +344,18 @@
     for f in range(frames):
         sums_scr[0, f] = jnp.where(rank == 0, state_of(0, f), 0.0)
 
-    def put_first(t, f, value):
-        first_scr[t, (f + 1) * hidden : (f + 2) * hidden, :] = value
-
-    def get_firsts(t, frame):
-        return first_scr[t, frame * hidden : (frame + 3) * hidden, :]
-
-    def add_drift(t, frame, step):
-        sums_scr[t + 1, frame] = sums_scr[t, frame] + step
+    def put_first(t, f, value, row, half):
+        start = (f + 1) * hidden + row
+        first_scr[t, start : start + PIECE, half] = value
+
+    def first_at(t, f, start, stop, half):
+        return first_scr[t, (f + 1) * hidden + start : (f + 1) * hidden + stop, half]
+
+    def add_drift(t, frame, step, half):
+        sums_scr[t + 1, frame, :, half] = sums_scr[t, frame, :, half] + step
 
     stage(1, [(t, f) for t in range(times) for f in range(frames)],
-          latent_of, lambda f: edge_flag(f, frames), put_first, get_firsts, add_drift, (),
+          latent_of, lambda f: edge_flag(f, frames), put_first, first_at, add_drift, (),
           steps_ref, spatial_ref, temporal_ref, out_weight_ref)
     for f in range(frames):
         deliver(picks_ref[1], times, f, lambda k, f=f: sums_scr[k, f], own_ref, send_ref)
@@ -272,7 +365,8 @@
     times, frames, channels, cells = window_states.shape
     hidden, taps = spatial_weight.shape
     slabs, ranks = lax.axis_size("slab"), lax.axis_size("tm")
-    assert ranks == 2 and EXTRA == 2 * ITERS * times and frames >= 3 and cells == HEIGHT * WIDTH
+    assert ranks == 2 and EXTRA == 2 * ITERS * times and hidden % PIECE == 0
+    assert taps - taps % LANES + LANES == TILE and frames >= 3 and cells == HEIGHT * WIDTH
     plane = (channels, cells)
     weights = (spatial_weight.T, temporal_weight, time_embed.T, out_weight)
     edge = pltpu.VMEM((times + 1, HALO) + plane, BF)
@@ -296,11 +390,12 @@
     scalars = (picks, steps)
     from_left = lax.ppermute(high, "slab", [(i, i + 1) for i in range(slabs - 1)])
     from_right = lax.ppermute(low, "slab", [(i + 1, i) for i in range(slabs - 1)])
-    spatial, temporal, firsts, inner = call(
+    spatial, temporal, project, firsts, inner = call(
         inner_first, "inner_first",
         (
-            ((hidden, taps + EXTRA), BF),
-            ((hidden, 3 * hidden), BF),
+            ((hidden, TILE), BF),
+            ((hidden, pl.cdiv(3 * hidden, TILE) * TILE), BF),
+            ((channels, pl.cdiv(hidden, TILE) * TILE), BF),
             ((times, frames * hidden, cells), BF),
             ((times + 1, frames - 2) + plane, F32),
         ),

time: 37.5 us -> 36.5 us (0.973)
  Pallas kernels: 25.4 us -> 24.5 us
    pallas_call x3, Pallas kernels: 23.6 us -> 22.7 us  [call(): pl.pallas_call(body, out_shape=tuple((pltpu.VMEM(dims, dtype) for dims, d...]
where the time goes in v4:
time: 36.5 us; the launch traced here: 36.4 us
  Pallas kernels  24.5 us (67%)
  starting transfers between devices  7.28 us (20%)
  waiting for transfers between devices  3.69 us (10%)
  other arithmetic  0.87 us (2%)
    pallas_call x3, Pallas kernels, call(): pl.pallas_call(body, out_shape=tuple((pltpu.VMEM(dims, dtype) for dims, d...  22.7 us
    ppermute x1, starting transfers between devices, local(): lax.ppermute(high, 'slab', [(i, i + 1) for i in range(slabs - 1)])  3.15 us
    ppermute x1, starting transfers between devices, local(): lax.ppermute(low, 'slab', [(i + 1, i) for i in range(slabs - 1)])  3.03 us
    pallas_call x1, Pallas kernels, local(): pl.pallas_call(load, out_shape=(*[pltpu.VMEM(x.shape, x.dtype) for x in w...  1.81 us
    ppermute x1, waiting for transfers between devices, local(): return mine + lax.ppermute(sent, 'tm', swap)  1.55 us
    ppermute x1, waiting for transfers between devices, local(): other = lax.ppermute(sent, 'tm', swap)  1.49 us
    add x1, other arithmetic, local(): return mine + lax.ppermute(sent, 'tm', swap)  0.87 us
  transfers between devices with their start and end apart: 4, of which 3 were waited for; matrix products, arithmetic and copies ran while one was open for 0% of the time, Pallas kernels for 15%

profile of v4, /device:TPU:19, one launch (start us, length us, event | category | flops | bytes accessed | tf_op | source)
XLA Modules:
  0.0 36.4 jit_solution(13811097437399124262)
XLA Ops:
  0.0 1.8 %load.1 = (bf16[144,320]{1,0:T(8,128)(2,1)S(1)}, bf16[3,320,320]{2,1,0:T(8,128)(2,1)S(1)}, f32[320,1000]{1,0:T(8,128)S(1)}, bf16[16,320]{1,0:T(8,128)(2,1)S(1)},...) custom-call(f32[4,4,16,512]{3,2,1,0:T(8,128)} %states_ref.1, ...), custom_call_target="tpu_custom_call" | custom-call | tf_op jit(solution)/shard_map/load/pallas_call | solution.py:373
  1.8 3.1 %collective-permute-start = (bf16[5,2,16,512]{3,2,1,0:T(8,128)(2,1)S(1)}, bf16[5,2,16,512]{3,2,1,0:T(8,128)(2,1)S(1)}, u32[]{:S(2)}, u32[]{:S(2)}) collective-permute-start(bf16[5,2,16,512]{3,2,1,0:T(8,128)(2,1)S(1)} %get-tuple-element.33), channel_id=1, source_target_pairs={{0,1},{1,2},{2,3},{3,4},{4,5},{5,6},{6,7},{8,9},{9,10},{10,11},{11... | collective-permute-start | bytes 491528 | tf_op jit(solution)/shard_map/ppermute | solution.py:391
  5.0 3.0 %collective-permute-start.1 = (bf16[5,2,16,512]{3,2,1,0:T(8,128)(2,1)S(1)}, bf16[5,2,16,512]{3,2,1,0:T(8,128)(2,1)S(1)}, u32[]{:S(2)}, u32[]{:S(2)}) collective-permute-start(bf16[5,2,16,512]{3,2,1,0:T(8,128)(2,1)S(1)} %get-tuple-element.34), channel_id=1, source_target_pairs={{1,0},{2,1},{3,2},{4,3},{5,4},{6,5},{7,6},{9,8},{10,9},{11,10},{12... | collective-permute-start | bytes 491528 | tf_op jit(solution)/shard_map/ppermute | solution.py:392
  8.0 5.5 %inner_first.1 = (bf16[320,256]{1,0:T(8,128)(2,1)S(1)}, bf16[320,1024]{1,0:T(8,128)(2,1)S(1)}, bf16[16,512]{1,0:T(8,128)(2,1)S(1)}, bf16[4,1280,512]{2,1,0:T(8,128)(2,1)S(1)}, f32[5,2,16,512]{3,2,1,0:T(8,128)S(1)}) custom-call(s32[10]{0:T(128)S(4)} %get-tuple-element.23.picks_ref, f32[8]{0:T(128)S(4)} %get-tuple-element.24.steps_ref, ...), custom_call_target="tpu_custom_call" | custom-call | tf_op jit(solution)/shard_map/inner_first/pallas_call | solution.py:29
  13.5 0.0 collective-permute-done.left_ref
  13.5 0.7 %collective-permute-done.1.right_ref = bf16[5,2,16,512]{3,2,1,0:T(8,128)(2,1)S(1)} collective-permute-done((bf16[5,2,16,512]{3,2,1,0:T(8,128)(2,1)S(1)}, bf16[5,2,16,512]{3,2,1,0:T(8,128)(2,1)S(1)}, u32[]{:S(2)}, u32[]{:S(2)}) %collective-permute-start.1) | collective-permute-done | bytes 163872 | tf_op jit(solution)/shard_map/ppermute | solution.py:392
  14.2 7.9 %outer_first.1 = (f32[4,6,16,512]{3,2,1,0:T(8,128)S(1)}, bf16[5,6,16,512]{3,2,1,0:T(8,128)(2,1)S(1)}) custom-call(s32[10]{0:T(128)S(4)} %get-tuple-element.23.picks_ref, f32[8]{0:T(128)S(4)} %get-tuple-element.24.steps_ref, bf16[320,256]{1,0:T(8,128)(2,1)S(1)} %get-tuple-element.30.spatial_ref, bf16[320,1024]{1,0:T(8,128)(2,1)S(1)} %get-tuple-element.31.temporal_ref, ...), custom_call_target="tpu_custom_call" | custom-call | tf_op jit(solution)/shard_map/outer_first/pallas_call | solution.py:29
  22.1 0.7 %collective-permute-start.2 = (bf16[5,6,16,512]{3,2,1,0:T(8,128)(2,1)S(1)}, bf16[5,6,16,512]{3,2,1,0:T(8,128)(2,1)S(1)}, u32[]{:S(2)}, u32[]{:S(2)}) collective-permute-start(bf16[5,6,16,512]{3,2,1,0:T(8,128)(2,1)S(1)} %get-tuple-element.38), channel_id=1, source_target_pairs={{0,8},{8,0},{1,9},{9,1},{2,10},{10,2},{3,11},{11,3},{4,12},{12,4},... | collective-permute-start | bytes 1474568 | tf_op jit(solution)/shard_map/ppermute | solution.py:412
  22.8 1.5 %collective-permute-done.2.other_ref = bf16[5,6,16,512]{3,2,1,0:T(8,128)(2,1)S(1)} collective-permute-done((bf16[5,6,16,512]{3,2,1,0:T(8,128)(2,1)S(1)}, bf16[5,6,16,512]{3,2,1,0:T(8,128)(2,1)S(1)}, u32[]{:S(2)}, u32[]{:S(2)}) %collective-permute-start.2) | collective-permute-done | bytes 491552 | tf_op jit(solution)/shard_map/ppermute | solution.py:412
  24.3 9.2 %second.1 = (f32[4,4,16,512]{3,2,1,0:T(8,128)S(1)}, f32[4,4,16,512]{3,2,1,0:T(8,128)S(1)}) custom-call(s32[10]{0:T(128)S(4)} %get-tuple-element.23.picks_ref, f32[8]{0:T(128)S(4)} %get-tuple-element.24.steps_ref, bf16[320,256]{1,0:T(8,128)(2,1)S(1)} %get-tuple-element.30.spatial_ref, bf16[320,1024]{1,0:T(8,128)(2,1)S(1)} %get-tuple-element.31.temporal_ref, ...), custom_call_target="tpu_custom_call" | custom-call | tf_op jit(solution)/shard_map/second/pallas_call | solution.py:29
  33.5 0.4 %collective-permute-start.3 = (f32[4,4,16,512]{3,2,1,0:T(8,128)S(1)}, f32[4,4,16,512]{3,2,1,0:T(8,128)S(1)}, u32[]{:S(2)}, u32[]{:S(2)}) collective-permute-start(f32[4,4,16,512]{3,2,1,0:T(8,128)S(1)} %get-tuple-element.40), channel_id=1, source_target_pairs={{0,8},{8,0},{1,9},{9,1},{2,10},{10,2},{3,11},{11,3},{4,12},{12,4},... | collective-permute-start | bytes 1572872 | tf_op jit(solution)/shard_map/ppermute | solution.py:418
  33.9 1.5 %collective-permute-done.3 = f32[4,4,16,512]{3,2,1,0:T(8,128)S(1)} collective-permute-done((f32[4,4,16,512]{3,2,1,0:T(8,128)S(1)}, f32[4,4,16,512]{3,2,1,0:T(8,128)S(1)}, u32[]{:S(2)}, u32[]{:S(2)}) %collective-permute-start.3) | collective-permute-done | bytes 524320 | tf_op jit(solution)/shard_map/ppermute | solution.py:418
  35.5 0.9 %add.3 = f32[4,4,16,512]{3,2,1,0:T(8,128)} add(f32[4,4,16,512]{3,2,1,0:T(8,128)S(1)} %get-tuple-element.39, f32[4,4,16,512]{3,2,1,0:T(8,128)S(1)} %collective-permute-done.3) | non-fusion elementwise | flops 131072 | bytes 1572864 | tf_op jit(solution)/shard_map/add | solution.py:418
Async XLA Ops:
  1.8 11.7 %collective-permute-start = (bf16[5,2,16,512]{3,2,1,0:T(8,128)(2,1)S(1)}, bf16[5,2,16,512]{3,2,1,0:T(8,128)(2,1)S(1)}, u32[]{:S(2)}, u32[]{:S(2)}) collective-permute-start(bf16[5,2,16,512]{3,2,1,0:T(8,128)(2,1)S(1)} %get-tuple-element.33), channel_id=1, source_target_pairs={{0,1},{1,2},{2,3},{3,4},{4,5},{5,6},{6,7},{8,9},{9,10},{10,11},{11... | collective-permute-start | bytes 491528 | tf_op jit(solution)/shard_map/ppermute | solution.py:391
  5.0 9.2 %collective-permute-start.1 = (bf16[5,2,16,512]{3,2,1,0:T(8,128)(2,1)S(1)}, bf16[5,2,16,512]{3,2,1,0:T(8,128)(2,1)S(1)}, u32[]{:S(2)}, u32[]{:S(2)}) collective-permute-start(bf16[5,2,16,512]{3,2,1,0:T(8,128)(2,1)S(1)} %get-tuple-element.34), channel_id=1, source_target_pairs={{1,0},{2,1},{3,2},{4,3},{5,4},{6,5},{7,6},{9,8},{10,9},{11,10},{12... | collective-permute-start | bytes 491528 | tf_op jit(solution)/shard_map/ppermute | solution.py:392
  22.1 2.2 %collective-permute-start.2 = (bf16[5,6,16,512]{3,2,1,0:T(8,128)(2,1)S(1)}, bf16[5,6,16,512]{3,2,1,0:T(8,128)(2,1)S(1)}, u32[]{:S(2)}, u32[]{:S(2)}) collective-permute-start(bf16[5,6,16,512]{3,2,1,0:T(8,128)(2,1)S(1)} %get-tuple-element.38), channel_id=1, source_target_pairs={{0,8},{8,0},{1,9},{9,1},{2,10},{10,2},{3,11},{11,3},{4,12},{12,4},... | collective-permute-start | bytes 1474568 | tf_op jit(solution)/shard_map/ppermute | solution.py:412
  33.5 2.0 %collective-permute-start.3 = (f32[4,4,16,512]{3,2,1,0:T(8,128)S(1)}, f32[4,4,16,512]{3,2,1,0:T(8,128)S(1)}, u32[]{:S(2)}, u32[]{:S(2)}) collective-permute-start(f32[4,4,16,512]{3,2,1,0:T(8,128)S(1)} %get-tuple-element.40), channel_id=1, source_target_pairs={{0,8},{8,0},{1,9},{9,1},{2,10},{10,2},{3,11},{11,3},{4,12},{12,4},... | collective-permute-start | bytes 1572872 | tf_op jit(solution)/shard_map/ppermute | solution.py:418

commit v5 on v4

--- a/solution.py
+++ b/solution.py
@@ -57,11 +57,11 @@
             steps_ref[sweep * times + i] = step_scr[index]
         picks_ref[sweep] = slides_scr[sweep]
     copies[3].wait()
-    for ref, first in ((low_ref, 0), (high_ref, frames - HALO)):
-        edge = states_out[:, first : first + HALO]
-        rounded = edge.astype(BF)
-        ref[:times] = rounded
-        ref[times] = (edge[0] - rounded[0].astype(F32)).astype(BF)
+    for ref, first, end in ((low_ref, 0, 0), (high_ref, frames - HALO, frames - 1)):
+        for t in range(times):
+            ref[t * HALO : (t + 1) * HALO] = states_out[t, first : first + HALO].astype(BF)
+        anchor = states_out[0, end]
+        ref[times * HALO] = (anchor - anchor.astype(BF).astype(F32)).astype(BF)
     for copy in copies[4:]:
         copy.wait()
 
@@ -70,18 +70,14 @@
     return half + half * jnp.tanh(half)
 
 
-def pack_weights(picks_ref, spatial_ref, temporal_ref, table_ref, spatial_out, temporal_out, project_ref, project_out, last_scr):
-    hidden = spatial_out.shape[0]
-    taps = spatial_ref.shape[0]
-    slots = EXTRA // 2
-    steps = table_ref.shape[1]
+def embed_columns(sweep, inset, times, picks_ref, table_ref, last_scr):
+    hidden, steps = table_ref.shape
     full = steps // LANES
     if steps % LANES:
         last_scr[:, : steps % LANES] = table_ref[:, full * LANES :]
     lane = lax.broadcasted_iota(jnp.int32, (1, LANES), 1)
-    inset = taps % LANES
     embed = jnp.zeros((hidden, LANES), F32)
-    for slot in range(slots):
+    for slot in range(sweep * times, (sweep + 1) * times):
         index = picks_ref[ITERS + slot]
         tile = index // LANES
         start = pl.multiple_of(jnp.minimum(tile, full - 1) * LANES, LANES)
@@ -93,10 +89,17 @@
         embed = jnp.where(lane == inset + slot, pltpu.roll(block, shift, 1), embed)
     embed = embed * 0.5
     rounded = embed.astype(BF).astype(F32)
-    extra = rounded + pltpu.roll(embed - rounded, slots, 1)
+    return (rounded + pltpu.roll(embed - rounded, EXTRA // 2, 1)).astype(BF)
+
+
+def pack_weights(picks_ref, spatial_ref, temporal_ref, table_ref, spatial_out, temporal_out, project_ref, project_out, last_scr):
+    hidden = spatial_out.shape[0]
+    taps = spatial_ref.shape[0]
+    inset = taps % LANES
+    times = EXTRA // 2 // ITERS
+    spatial_out[:, taps - inset :] = embed_columns(0, inset, times, picks_ref, table_ref, last_scr)
     weight = (spatial_ref[...].astype(F32) * 0.5).T.astype(BF)
     spatial_out[:, : taps - inset] = weight[:, : taps - inset]
-    spatial_out[:, taps - inset :] = extra.astype(BF)
     spatial_out[:, taps - inset : taps] = weight[:, taps - inset :]
     for lag in range(3):
         temporal_out[:, lag * hidden : (lag + 1) * hidden] = temporal_ref[lag] * 0.5
@@ -129,7 +132,7 @@
 
 
 def stage(sweep, items, latent_of, valid_of, put_first, first_at, add_drift, have,
-          steps_ref, spatial_ref, temporal_ref, project_ref):
+          steps_ref, spatial_ref, temporal_ref, project_ref, aside=None):
     times = EXTRA // 2 // ITERS
     hidden = spatial_ref.shape[0]
     pieces = hidden // PIECE
@@ -222,6 +225,8 @@
             if n > 1:
                 finish_project(n - 2)
             temporal(n, 2)
+            if n == len(items) // 2 and aside is not None:
+                aside()
             if n > 0:
                 project(second, 0)
             if early is not None:
@@ -285,8 +290,9 @@
             send_ref[times, frame] = (sent - sent.astype(BF).astype(F32)).astype(BF)
 
 
-def outer_first(picks_ref, steps_ref, spatial_ref, temporal_ref, out_weight_ref, states_ref,
-                left_ref, right_ref, first_ref, inner_ref, own_ref, send_ref, first_scr, sums_scr):
+def outer_first(picks_ref, steps_ref, spatial_ref, temporal_ref, out_weight_ref, table_ref, states_ref,
+                left_ref, right_ref, first_ref, inner_ref,
+                own_ref, send_ref, later_ref, first_scr, sums_scr, last_scr):
     times, frames = states_ref.shape[0], states_ref.shape[1]
     hidden = temporal_ref.shape[0]
     rank = lax.axis_index("tm")
@@ -294,13 +300,14 @@
     halo = [-2, -1, frames, frames + 1]
 
     def latent_of(t, f):
-        return left_ref[t, f + HALO] if f < 0 else right_ref[t, f - frames]
+        return left_ref[t * HALO + f + HALO] if f < 0 else right_ref[t * HALO + f - frames]
 
     for n, f in enumerate(outs):
         if 0 <= f < frames:
             state = states_ref[0, f]
         else:
-            state = latent_of(0, f).astype(F32) + latent_of(times, f).astype(F32)
+            rest = left_ref if f < 0 else right_ref
+            state = latent_of(0, f).astype(F32) + rest[times * HALO].astype(F32)
         sums_scr[0, n] = jnp.where(rank == 0, state, 0.0)
 
     def put_first(t, f, value, row, half):
@@ -317,9 +324,17 @@
         n = outs.index(frame)
         sums_scr[t + 1, n, :, half] = sums_scr[t, n, :, half] + step
 
+    def next_embeddings():
+        taps = 9 * states_ref.shape[2]
+        inset = taps % LANES
+        columns = embed_columns(1, inset, times, picks_ref, table_ref, last_scr)
+        lane = lax.broadcasted_iota(jnp.int32, (1, LANES), 1)
+        later_ref[:, : taps - inset] = spatial_ref[:, : taps - inset]
+        later_ref[:, taps - inset :] = jnp.where(lane < inset, spatial_ref[:, taps - inset :], columns)
+
     stage(0, [(t, f) for t in range(times) for f in outs],
           latent_of, lambda f: edge_flag(f, frames), put_first, first_at, add_drift, range(frames),
-          steps_ref, spatial_ref, temporal_ref, out_weight_ref)
+          steps_ref, spatial_ref, temporal_ref, out_weight_ref, next_embeddings)
     for f in range(-1, frames + 1):
         sums = (lambda k, n=outs.index(f): sums_scr[k, n]) if f in outs else (lambda k, f=f: inner_ref[k, f - 1])
         deliver(picks_ref[0], times, f + 1, sums, own_ref, send_ref)
@@ -369,7 +384,7 @@
     assert taps - taps % LANES + LANES == TILE and frames >= 3 and cells == HEIGHT * WIDTH
     plane = (channels, cells)
     weights = (spatial_weight.T, temporal_weight, time_embed.T, out_weight)
-    edge = pltpu.VMEM((times + 1, HALO) + plane, BF)
+    edge = pltpu.VMEM((times * HALO + 1,) + plane, BF)
     *weights, states, low, high, picks, steps = pl.pallas_call(
         load,
         out_shape=(
@@ -403,16 +418,19 @@
         [pltpu.VMEM((hidden, LANES), F32)], 16,
     )
     wide = ((times, frames + 2) + plane, F32)
-    mine, sent = call(
-        outer_first, "outer_first", (wide, ((times + 1, frames + 2) + plane, BF)), scalars,
-        (spatial, temporal, project, states, from_left, from_right, firsts, inner),
-        [pltpu.VMEM((times, 4 * hidden, cells), BF), pltpu.VMEM((times + 1, 4) + plane, F32)], 16,
+    mine, sent, later = call(
+        outer_first, "outer_first", (wide, ((times + 1, frames + 2) + plane, BF), ((hidden, TILE), BF)), scalars,
+        (spatial, temporal, project, table, states, from_left, from_right, firsts, inner),
+        [
+            pltpu.VMEM((times, 4 * hidden, cells), BF), pltpu.VMEM((times + 1, 4) + plane, F32),
+            pltpu.VMEM((hidden, LANES), F32),
+        ], 16,
     )
     swap = [(0, 1), (1, 0)]
     other = lax.ppermute(sent, "tm", swap)
     block = ((times, frames) + plane, F32)
     mine, sent = call(
-        second, "second", (block, block), scalars, (spatial, temporal, project, mine, other),
+        second, "second", (block, block), scalars, (later, temporal, project, mine, other),
         [pltpu.VMEM((times, (frames + 2) * hidden, cells), BF), pltpu.VMEM((times + 1, frames) + plane, F32)], 24,
     )
     return mine + lax.ppermute(sent, "tm", swap)

time: 36.5 us -> 36.1 us (0.989)
  waiting for transfers between devices: 3.69 us -> 3.05 us
  starting transfers between devices: 7.28 us -> 7.92 us
  Pallas kernels: 24.5 us -> 24 us
    ppermute x1, waiting for transfers between devices: 0.65 us -> 0.01 us  [local(): lax.ppermute(low, 'slab', [(i + 1, i) for i in range(slabs - 1)])]
    ppermute x1, starting transfers between devices: 0.67 us -> 1.31 us  [local(): other = lax.ppermute(sent, 'tm', swap)]
    pallas_call x3, Pallas kernels: 22.7 us -> 22.2 us  [call(): pl.pallas_call(body, out_shape=tuple((pltpu.VMEM(dims, dtype) for dims, d...]
  transfers between devices with their start and end apart: 4 -> 4, of which waited for: 3 -> 2; matrix products, arithmetic and copies ran while one was open for 0% -> 0% of each run, Pallas kernels for 15% -> 15%
where the time goes in v5:
time: 36.1 us; the launch traced here: 35.9 us
  Pallas kernels  24 us (66%)
  starting transfers between devices  7.92 us (22%)
  waiting for transfers between devices  3.05 us (8%)
  other arithmetic  0.87 us (2%)
    pallas_call x3, Pallas kernels, call(): pl.pallas_call(body, out_shape=tuple((pltpu.VMEM(dims, dtype) for dims, d...  22.2 us
    ppermute x1, starting transfers between devices, local(): lax.ppermute(high, 'slab', [(i, i + 1) for i in range(slabs - 1)])  3.15 us
    ppermute x1, starting transfers between devices, local(): lax.ppermute(low, 'slab', [(i + 1, i) for i in range(slabs - 1)])  3.03 us
    pallas_call x1, Pallas kernels, local(): pl.pallas_call(load, out_shape=(*[pltpu.VMEM(x.shape, x.dtype) for x in w...  1.81 us
    ppermute x1, waiting for transfers between devices, local(): return mine + lax.ppermute(sent, 'tm', swap)  1.55 us
    ppermute x1, waiting for transfers between devices, local(): other = lax.ppermute(sent, 'tm', swap)  1.49 us
    ppermute x1, starting transfers between devices, local(): other = lax.ppermute(sent, 'tm', swap)  1.31 us
    add x1, other arithmetic, local(): return mine + lax.ppermute(sent, 'tm', swap)  0.87 us
  transfers between devices with their start and end apart: 4, of which 2 were waited for; matrix products, arithmetic and copies ran while one was open for 0% of the time, Pallas kernels for 15%

profile of v5, /device:TPU:19, one launch (start us, length us, event | category | flops | bytes accessed | tf_op | source)
XLA Modules:
  0.0 35.9 jit_solution(7065468620849002569)
XLA Ops:
  0.0 1.8 %load.1 = (bf16[144,320]{1,0:T(8,128)(2,1)S(1)}, bf16[3,320,320]{2,1,0:T(8,128)(2,1)S(1)}, f32[320,1000]{1,0:T(8,128)S(1)}, bf16[16,320]{1,0:T(8,128)(2,1)S(1)},...) custom-call(f32[4,4,16,512]{3,2,1,0:T(8,128)} %states_ref.1, ...), custom_call_target="tpu_custom_call" | custom-call | tf_op jit(solution)/shard_map/load/pallas_call | solution.py:388
  1.8 3.1 %collective-permute-start = (bf16[9,16,512]{2,1,0:T(8,128)(2,1)S(1)}, bf16[9,16,512]{2,1,0:T(8,128)(2,1)S(1)}, u32[]{:S(2)}, u32[]{:S(2)}) collective-permute-start(bf16[9,16,512]{2,1,0:T(8,128)(2,1)S(1)} %get-tuple-element.34), channel_id=1, source_target_pairs={{0,1},{1,2},{2,3},{3,4},{4,5},{5,6},{6,7},{8,9},{9,10},{10,11},{11... | collective-permute-start | bytes 442376 | tf_op jit(solution)/shard_map/ppermute | solution.py:406
  5.0 3.0 %collective-permute-start.1 = (bf16[9,16,512]{2,1,0:T(8,128)(2,1)S(1)}, bf16[9,16,512]{2,1,0:T(8,128)(2,1)S(1)}, u32[]{:S(2)}, u32[]{:S(2)}) collective-permute-start(bf16[9,16,512]{2,1,0:T(8,128)(2,1)S(1)} %get-tuple-element.35), channel_id=1, source_target_pairs={{1,0},{2,1},{3,2},{4,3},{5,4},{6,5},{7,6},{9,8},{10,9},{11,10},{12... | collective-permute-start | bytes 442376 | tf_op jit(solution)/shard_map/ppermute | solution.py:407
  8.0 5.2 %inner_first.1 = (bf16[320,256]{1,0:T(8,128)(2,1)S(1)}, bf16[320,1024]{1,0:T(8,128)(2,1)S(1)}, bf16[16,512]{1,0:T(8,128)(2,1)S(1)}, bf16[4,1280,512]{2,1,0:T(8,128)(2,1)S(1)}, f32[5,2,16,512]{3,2,1,0:T(8,128)S(1)}) custom-call(s32[10]{0:T(128)S(4)} %get-tuple-element.24.picks_ref, f32[8]{0:T(128)S(4)} %get-tuple-element.25.steps_ref, ...), custom_call_target="tpu_custom_call" | custom-call | tf_op jit(solution)/shard_map/inner_first/pallas_call | solution.py:29
  13.3 0.0 collective-permute-done.left_ref
  13.3 0.0 collective-permute-done.1.right_ref
  13.3 7.9 %outer_first.1 = (f32[4,6,16,512]{3,2,1,0:T(8,128)S(1)}, bf16[5,6,16,512]{3,2,1,0:T(8,128)(2,1)S(1)}, bf16[320,256]{1,0:T(8,128)(2,1)S(1)}) custom-call(s32[10]{0:T(128)S(4)} %get-tuple-element.24.picks_ref, f32[8]{0:T(128)S(4)} %get-tuple-element.25.steps_ref, bf16[320,256]{1,0:T(8,128)(2,1)S(1)} %get-tuple-element.31.spatial_ref, ...), custom_call_target="tpu_custom_call" | custom-call | tf_op jit(solution)/shard_map/outer_first/pallas_call | solution.py:29
  21.2 1.3 %collective-permute-start.2 = (bf16[5,6,16,512]{3,2,1,0:T(8,128)(2,1)S(1)}, bf16[5,6,16,512]{3,2,1,0:T(8,128)(2,1)S(1)}, u32[]{:S(2)}, u32[]{:S(2)}) collective-permute-start(bf16[5,6,16,512]{3,2,1,0:T(8,128)(2,1)S(1)} %get-tuple-element.40), channel_id=1, source_target_pairs={{0,8},{8,0},{1,9},{9,1},{2,10},{10,2},{3,11},{11,3},{4,12},{12,4},... | collective-permute-start | bytes 1474568 | tf_op jit(solution)/shard_map/ppermute | solution.py:430
  22.5 1.5 %collective-permute-done.2.other_ref = bf16[5,6,16,512]{3,2,1,0:T(8,128)(2,1)S(1)} collective-permute-done((bf16[5,6,16,512]{3,2,1,0:T(8,128)(2,1)S(1)}, bf16[5,6,16,512]{3,2,1,0:T(8,128)(2,1)S(1)}, u32[]{:S(2)}, u32[]{:S(2)}) %collective-permute-start.2) | collective-permute-done | bytes 491552 | tf_op jit(solution)/shard_map/ppermute | solution.py:430
  24.0 9.1 %second.1 = (f32[4,4,16,512]{3,2,1,0:T(8,128)S(1)}, f32[4,4,16,512]{3,2,1,0:T(8,128)S(1)}) custom-call(s32[10]{0:T(128)S(4)} %get-tuple-element.24.picks_ref, f32[8]{0:T(128)S(4)} %get-tuple-element.25.steps_ref, bf16[320,256]{1,0:T(8,128)(2,1)S(1)} %get-tuple-element.38.spatial_ref, bf16[320,1024]{1,0:T(8,128)(2,1)S(1)} %get-tuple-element.32.temporal_ref, ...), custom_call_target="tpu_custom_call" | custom-call | tf_op jit(solution)/shard_map/second/pallas_call | solution.py:29
  33.1 0.4 %collective-permute-start.3 = (f32[4,4,16,512]{3,2,1,0:T(8,128)S(1)}, f32[4,4,16,512]{3,2,1,0:T(8,128)S(1)}, u32[]{:S(2)}, u32[]{:S(2)}) collective-permute-start(f32[4,4,16,512]{3,2,1,0:T(8,128)S(1)} %get-tuple-element.42), channel_id=1, source_target_pairs={{0,8},{8,0},{1,9},{9,1},{2,10},{10,2},{3,11},{11,3},{4,12},{12,4},... | collective-permute-start | bytes 1572872 | tf_op jit(solution)/shard_map/ppermute | solution.py:436
  33.5 1.5 %collective-permute-done.3 = f32[4,4,16,512]{3,2,1,0:T(8,128)S(1)} collective-permute-done((f32[4,4,16,512]{3,2,1,0:T(8,128)S(1)}, f32[4,4,16,512]{3,2,1,0:T(8,128)S(1)}, u32[]{:S(2)}, u32[]{:S(2)}) %collective-permute-start.3) | collective-permute-done | bytes 524320 | tf_op jit(solution)/shard_map/ppermute | solution.py:436
  35.0 0.9 %add.3 = f32[4,4,16,512]{3,2,1,0:T(8,128)} add(f32[4,4,16,512]{3,2,1,0:T(8,128)S(1)} %get-tuple-element.41, f32[4,4,16,512]{3,2,1,0:T(8,128)S(1)} %collective-permute-done.3) | non-fusion elementwise | flops 131072 | bytes 1572864 | tf_op jit(solution)/shard_map/add | solution.py:436
Async XLA Ops:
  1.8 11.4 %collective-permute-start = (bf16[9,16,512]{2,1,0:T(8,128)(2,1)S(1)}, bf16[9,16,512]{2,1,0:T(8,128)(2,1)S(1)}, u32[]{:S(2)}, u32[]{:S(2)}) collective-permute-start(bf16[9,16,512]{2,1,0:T(8,128)(2,1)S(1)} %get-tuple-element.34), channel_id=1, source_target_pairs={{0,1},{1,2},{2,3},{3,4},{4,5},{5,6},{6,7},{8,9},{9,10},{10,11},{11... | collective-permute-start | bytes 442376 | tf_op jit(solution)/shard_map/ppermute | solution.py:406
  5.0 8.3 %collective-permute-start.1 = (bf16[9,16,512]{2,1,0:T(8,128)(2,1)S(1)}, bf16[9,16,512]{2,1,0:T(8,128)(2,1)S(1)}, u32[]{:S(2)}, u32[]{:S(2)}) collective-permute-start(bf16[9,16,512]{2,1,0:T(8,128)(2,1)S(1)} %get-tuple-element.35), channel_id=1, source_target_pairs={{1,0},{2,1},{3,2},{4,3},{5,4},{6,5},{7,6},{9,8},{10,9},{11,10},{12... | collective-permute-start | bytes 442376 | tf_op jit(solution)/shard_map/ppermute | solution.py:407
  21.2 2.8 %collective-permute-start.2 = (bf16[5,6,16,512]{3,2,1,0:T(8,128)(2,1)S(1)}, bf16[5,6,16,512]{3,2,1,0:T(8,128)(2,1)S(1)}, u32[]{:S(2)}, u32[]{:S(2)}) collective-permute-start(bf16[5,6,16,512]{3,2,1,0:T(8,128)(2,1)S(1)} %get-tuple-element.40), channel_id=1, source_target_pairs={{0,8},{8,0},{1,9},{9,1},{2,10},{10,2},{3,11},{11,3},{4,12},{12,4},... | collective-permute-start | bytes 1474568 | tf_op jit(solution)/shard_map/ppermute | solution.py:430
  33.1 2.0 %collective-permute-start.3 = (f32[4,4,16,512]{3,2,1,0:T(8,128)S(1)}, f32[4,4,16,512]{3,2,1,0:T(8,128)S(1)}, u32[]{:S(2)}, u32[]{:S(2)}) collective-permute-start(f32[4,4,16,512]{3,2,1,0:T(8,128)S(1)} %get-tuple-element.42), channel_id=1, source_target_pairs={{0,8},{8,0},{1,9},{9,1},{2,10},{10,2},{3,11},{11,3},{4,12},{12,4},... | collective-permute-start | bytes 1572872 | tf_op jit(solution)/shard_map/ppermute | solution.py:436

commit v6 on v5

--- a/solution.py
+++ b/solution.py
@@ -374,6 +374,17 @@
           steps_ref, spatial_ref, temporal_ref, out_weight_ref)
     for f in range(frames):
         deliver(picks_ref[1], times, f, lambda k, f=f: sums_scr[k, f], own_ref, send_ref)
+
+
+def combine(mine_ref, other_ref, out_ref, sum_scr, sems):
+    copies = []
+    for j in range(mine_ref.shape[0]):
+        sum_scr[j] = mine_ref[j] + other_ref[j]
+        copy = pltpu.make_async_copy(sum_scr.at[j], out_ref.at[j], sems.at[j])
+        copy.start()
+        copies.append(copy)
+    for copy in copies:
+        copy.wait()
 
 
 def local(window_states, spatial_weight, temporal_weight, out_weight, time_embed, step_size, time_index, slides):
@@ -433,7 +444,16 @@
         second, "second", (block, block), scalars, (later, temporal, project, mine, other),
         [pltpu.VMEM((times, (frames + 2) * hidden, cells), BF), pltpu.VMEM((times + 1, frames) + plane, F32)], 24,
     )
-    return mine + lax.ppermute(sent, "tm", swap)
+    other = lax.ppermute(sent, "tm", swap)
+    return pl.pallas_call(
+        combine,
+        out_shape=jax.ShapeDtypeStruct(window_states.shape, F32),
+        in_specs=[VMEM, VMEM],
+        out_specs=HBM,
+        scratch_shapes=[pltpu.VMEM(window_states.shape, F32), pltpu.SemaphoreType.DMA((times,))],
+        compiler_params=pltpu.CompilerParams(vmem_limit_bytes=4 * MIB),
+        name="combine",
+    )(kept(mine), kept(other))
 
 
 def solution(mesh):

time: 36.1 us -> 36.2 us (level)
  other arithmetic: 0.87 us -> 0 us
  Pallas kernels: 24 us -> 24.8 us
    ppermute x1 -> x0, waiting for transfers between devices: 1.55 us -> none  [local(): return mine + lax.ppermute(sent, 'tm', swap)]
    ppermute x1 -> x2, waiting for transfers between devices: 1.49 us -> 3.03 us  [local(): other = lax.ppermute(sent, 'tm', swap)]
    add x1 -> x0, other arithmetic: 0.87 us -> none  [local(): return mine + lax.ppermute(sent, 'tm', swap)]
    pallas_call x0 -> x1, Pallas kernels: none -> 0.83 us  [local(): pl.pallas_call(combine, out_shape=jax.ShapeDtypeStruct(window_states.shap...]
    ppermute x1 -> x2, starting transfers between devices: 1.31 us -> 1.76 us  [local(): other = lax.ppermute(sent, 'tm', swap)]
    ppermute x1 -> x0, starting transfers between devices: 0.43 us -> none  [local(): return mine + lax.ppermute(sent, 'tm', swap)]
where the time goes in v6:
time: 36.2 us; the launch traced here: 36 us
  Pallas kernels  24.8 us (69%)
  starting transfers between devices  7.94 us (22%)
  waiting for transfers between devices  3.04 us (8%)
    pallas_call x3, Pallas kernels, call(): pl.pallas_call(body, out_shape=tuple((pltpu.VMEM(dims, dtype) for dims, d...  22.2 us
    ppermute x1, starting transfers between devices, local(): lax.ppermute(high, 'slab', [(i, i + 1) for i in range(slabs - 1)])  3.15 us
    ppermute x1, starting transfers between devices, local(): lax.ppermute(low, 'slab', [(i + 1, i) for i in range(slabs - 1)])  3.03 us
    ppermute x2, waiting for transfers between devices, local(): other = lax.ppermute(sent, 'tm', swap)  3.03 us
    pallas_call x1, Pallas kernels, local(): pl.pallas_call(load, out_shape=(*[pltpu.VMEM(x.shape, x.dtype) for x in w...  1.81 us
    ppermute x2, starting transfers between devices, local(): other = lax.ppermute(sent, 'tm', swap)  1.76 us
    pallas_call x1, Pallas kernels, local(): pl.pallas_call(combine, out_shape=jax.ShapeDtypeStruct(window_states.shap...  0.83 us
  transfers between devices with their start and end apart: 4, of which 2 were waited for; matrix products, arithmetic and copies ran while one was open for 0% of the time, Pallas kernels for 15%

profile of v6, /device:TPU:19, one launch (start us, length us, event | category | flops | bytes accessed | tf_op | source)
XLA Modules:
  0.0 36.0 jit_solution(8310451287421922977)
XLA Ops:
  0.0 1.8 %load.1 = (bf16[144,320]{1,0:T(8,128)(2,1)S(1)}, bf16[3,320,320]{2,1,0:T(8,128)(2,1)S(1)}, f32[320,1000]{1,0:T(8,128)S(1)}, bf16[16,320]{1,0:T(8,128)(2,1)S(1)},...) custom-call(f32[4,4,16,512]{3,2,1,0:T(8,128)} %states_ref.1, ...), custom_call_target="tpu_custom_call" | custom-call | tf_op jit(solution)/shard_map/load/pallas_call | solution.py:399
  1.8 3.1 %collective-permute-start = (bf16[9,16,512]{2,1,0:T(8,128)(2,1)S(1)}, bf16[9,16,512]{2,1,0:T(8,128)(2,1)S(1)}, u32[]{:S(2)}, u32[]{:S(2)}) collective-permute-start(bf16[9,16,512]{2,1,0:T(8,128)(2,1)S(1)} %get-tuple-element.34), channel_id=1, source_target_pairs={{0,1},{1,2},{2,3},{3,4},{4,5},{5,6},{6,7},{8,9},{9,10},{10,11},{11... | collective-permute-start | bytes 442376 | tf_op jit(solution)/shard_map/ppermute | solution.py:417
  5.0 3.0 %collective-permute-start.1 = (bf16[9,16,512]{2,1,0:T(8,128)(2,1)S(1)}, bf16[9,16,512]{2,1,0:T(8,128)(2,1)S(1)}, u32[]{:S(2)}, u32[]{:S(2)}) collective-permute-start(bf16[9,16,512]{2,1,0:T(8,128)(2,1)S(1)} %get-tuple-element.35), channel_id=1, source_target_pairs={{1,0},{2,1},{3,2},{4,3},{5,4},{6,5},{7,6},{9,8},{10,9},{11,10},{12... | collective-permute-start | bytes 442376 | tf_op jit(solution)/shard_map/ppermute | solution.py:418
  8.0 5.2 %inner_first.1 = (bf16[320,256]{1,0:T(8,128)(2,1)S(1)}, bf16[320,1024]{1,0:T(8,128)(2,1)S(1)}, bf16[16,512]{1,0:T(8,128)(2,1)S(1)}, bf16[4,1280,512]{2,1,0:T(8,128)(2,1)S(1)}, f32[5,2,16,512]{3,2,1,0:T(8,128)S(1)}) custom-call(s32[10]{0:T(128)S(4)} %get-tuple-element.24.picks_ref, f32[8]{0:T(128)S(4)} %get-tuple-element.25.steps_ref, ...), custom_call_target="tpu_custom_call" | custom-call | tf_op jit(solution)/shard_map/inner_first/pallas_call | solution.py:29
  13.3 0.0 collective-permute-done.left_ref
  13.3 0.0 collective-permute-done.1.right_ref
  13.3 7.9 %outer_first.1 = (f32[4,6,16,512]{3,2,1,0:T(8,128)S(1)}, bf16[5,6,16,512]{3,2,1,0:T(8,128)(2,1)S(1)}, bf16[320,256]{1,0:T(8,128)(2,1)S(1)}) custom-call(s32[10]{0:T(128)S(4)} %get-tuple-element.24.picks_ref, f32[8]{0:T(128)S(4)} %get-tuple-element.25.steps_ref, bf16[320,256]{1,0:T(8,128)(2,1)S(1)} %get-tuple-element.31.spatial_ref, ...), custom_call_target="tpu_custom_call" | custom-call | tf_op jit(solution)/shard_map/outer_first/pallas_call | solution.py:29
  21.2 1.3 %collective-permute-start.2 = (bf16[5,6,16,512]{3,2,1,0:T(8,128)(2,1)S(1)}, bf16[5,6,16,512]{3,2,1,0:T(8,128)(2,1)S(1)}, u32[]{:S(2)}, u32[]{:S(2)}) collective-permute-start(bf16[5,6,16,512]{3,2,1,0:T(8,128)(2,1)S(1)} %get-tuple-element.40), channel_id=1, source_target_pairs={{0,8},{8,0},{1,9},{9,1},{2,10},{10,2},{3,11},{11,3},{4,12},{12,4},... | collective-permute-start | bytes 1474568 | tf_op jit(solution)/shard_map/ppermute | solution.py:441
  22.5 1.5 %collective-permute-done.2.other_ref = bf16[5,6,16,512]{3,2,1,0:T(8,128)(2,1)S(1)} collective-permute-done((bf16[5,6,16,512]{3,2,1,0:T(8,128)(2,1)S(1)}, bf16[5,6,16,512]{3,2,1,0:T(8,128)(2,1)S(1)}, u32[]{:S(2)}, u32[]{:S(2)}) %collective-permute-start.2) | collective-permute-done | bytes 491552 | tf_op jit(solution)/shard_map/ppermute | solution.py:441
  24.0 9.1 %second.1 = (f32[4,4,16,512]{3,2,1,0:T(8,128)S(1)}, f32[4,4,16,512]{3,2,1,0:T(8,128)S(1)}) custom-call(s32[10]{0:T(128)S(4)} %get-tuple-element.24.picks_ref, f32[8]{0:T(128)S(4)} %get-tuple-element.25.steps_ref, bf16[320,256]{1,0:T(8,128)(2,1)S(1)} %get-tuple-element.38.spatial_ref, bf16[320,1024]{1,0:T(8,128)(2,1)S(1)} %get-tuple-element.32.temporal_ref, ...), custom_call_target="tpu_custom_call" | custom-call | tf_op jit(solution)/shard_map/second/pallas_call | solution.py:29
  33.1 0.4 %collective-permute-start.3 = (f32[4,4,16,512]{3,2,1,0:T(8,128)S(1)}, f32[4,4,16,512]{3,2,1,0:T(8,128)S(1)}, u32[]{:S(2)}, u32[]{:S(2)}) collective-permute-start(f32[4,4,16,512]{3,2,1,0:T(8,128)S(1)} %get-tuple-element.42), channel_id=1, source_target_pairs={{0,8},{8,0},{1,9},{9,1},{2,10},{10,2},{3,11},{11,3},{4,12},{12,4},... | collective-permute-start | bytes 1572872 | tf_op jit(solution)/shard_map/ppermute | solution.py:447
  33.5 1.5 %collective-permute-done.3.other_ref = f32[4,4,16,512]{3,2,1,0:T(8,128)S(1)} collective-permute-done((f32[4,4,16,512]{3,2,1,0:T(8,128)S(1)}, f32[4,4,16,512]{3,2,1,0:T(8,128)S(1)}, u32[]{:S(2)}, u32[]{:S(2)}) %collective-permute-start.3) | collective-permute-done | bytes 524320 | tf_op jit(solution)/shard_map/ppermute | solution.py:447
  35.0 0.8 %combine.1 = f32[4,4,16,512]{3,2,1,0:T(8,128)} custom-call(f32[4,4,16,512]{3,2,1,0:T(8,128)S(1)} %get-tuple-element.41.mine_ref, f32[4,4,16,512]{3,2,1,0:T(8,128)S(1)} %collective-permute-done.3.other_ref), custom_call_target="tpu_custom_call" | custom-call | tf_op jit(solution)/shard_map/combine/pallas_call | solution.py:448
Async XLA Ops:
  1.8 11.4 %collective-permute-start = (bf16[9,16,512]{2,1,0:T(8,128)(2,1)S(1)}, bf16[9,16,512]{2,1,0:T(8,128)(2,1)S(1)}, u32[]{:S(2)}, u32[]{:S(2)}) collective-permute-start(bf16[9,16,512]{2,1,0:T(8,128)(2,1)S(1)} %get-tuple-element.34), channel_id=1, source_target_pairs={{0,1},{1,2},{2,3},{3,4},{4,5},{5,6},{6,7},{8,9},{9,10},{10,11},{11... | collective-permute-start | bytes 442376 | tf_op jit(solution)/shard_map/ppermute | solution.py:417
  5.0 8.3 %collective-permute-start.1 = (bf16[9,16,512]{2,1,0:T(8,128)(2,1)S(1)}, bf16[9,16,512]{2,1,0:T(8,128)(2,1)S(1)}, u32[]{:S(2)}, u32[]{:S(2)}) collective-permute-start(bf16[9,16,512]{2,1,0:T(8,128)(2,1)S(1)} %get-tuple-element.35), channel_id=1, source_target_pairs={{1,0},{2,1},{3,2},{4,3},{5,4},{6,5},{7,6},{9,8},{10,9},{11,10},{12... | collective-permute-start | bytes 442376 | tf_op jit(solution)/shard_map/ppermute | solution.py:418
  21.2 2.8 %collective-permute-start.2 = (bf16[5,6,16,512]{3,2,1,0:T(8,128)(2,1)S(1)}, bf16[5,6,16,512]{3,2,1,0:T(8,128)(2,1)S(1)}, u32[]{:S(2)}, u32[]{:S(2)}) collective-permute-start(bf16[5,6,16,512]{3,2,1,0:T(8,128)(2,1)S(1)} %get-tuple-element.40), channel_id=1, source_target_pairs={{0,8},{8,0},{1,9},{9,1},{2,10},{10,2},{3,11},{11,3},{4,12},{12,4},... | collective-permute-start | bytes 1474568 | tf_op jit(solution)/shard_map/ppermute | solution.py:441
  33.1 2.0 %collective-permute-start.3 = (f32[4,4,16,512]{3,2,1,0:T(8,128)S(1)}, f32[4,4,16,512]{3,2,1,0:T(8,128)S(1)}, u32[]{:S(2)}, u32[]{:S(2)}) collective-permute-start(f32[4,4,16,512]{3,2,1,0:T(8,128)S(1)} %get-tuple-element.42), channel_id=1, source_target_pairs={{0,8},{8,0},{1,9},{9,1},{2,10},{10,2},{3,11},{11,3},{4,12},{12,4},... | collective-permute-start | bytes 1572872 | tf_op jit(solution)/shard_map/ppermute | solution.py:447
